TPU v7x, 256 devices: a whole 4x4x8 slice. The times are simulated.
256 devices in a mesh: fsdp: 16 (over z, core), cols: 16 (over y, x).
Axes of the slice: x: 4, y: 4, z: 8, core: 2. Of those that a mesh axis runs over, the one named last changes fastest.
Arguments:
- one_query: float32 [4096, 4096], P('fsdp', 'cols'), may hold values from -0.125 to 0.125
- other_query: float32 [4096, 4096], P('fsdp', 'cols'), may hold values from -0.09375 to 0.09375
- one_key: float32 [4096, 4096], P('fsdp', 'cols'), may hold values from -0.125 to 0.125
- other_key: float32 [4096, 4096], P('fsdp', 'cols'), may hold values from -0.09375 to 0.09375
- one_value: float32 [4096, 4096], P('fsdp', 'cols'), may hold values from -0.125 to 0.125
- other_value: float32 [4096, 4096], P('fsdp', 'cols'), may hold values from -0.09375 to 0.09375
- mix_share: float32 [4096], P('fsdp'), may hold values from 0.2 to 0.8
- norm_train: float32 [4096], P(('fsdp', 'cols')), may hold values from 0.25 to 1.75
- norm_step: float32 [4096], P(('fsdp', 'cols')), may hold values from -0.3 to 0.3
Outputs:
- final_query: bfloat16 [4096, 4096], P(None, 'cols')
- final_key: bfloat16 [4096, 4096], P(None, 'cols')
- final_value: bfloat16 [4096, 4096], P(None, 'cols')
- scale_query: float32 [4096], P('cols')
- scale_key: float32 [4096], P('cols')
- scale_value: float32 [4096], P('cols')
- serve_norm: bfloat16 [4096], replicated
All inputs are finite; a program needn't handle non-finite values.
Results may differ from a plain program's by a relative error of at most 0.0004.
Values may be sent and summed in bfloat16 or wider, within the bound.
A program may use at most 64 MiB of HBM per device.

v0:
```python
import jax
import jax.numpy as jnp
from jax import lax
from jax.sharding import Mesh
from jax.sharding import PartitionSpec as P

FSDP = ("fsdp_0", "fsdp_1")
FSDP_COLS = ("fsdp_0", "fsdp_1", "cols_0", "cols_1")
COLS = ("cols_0", "cols_1")


def copy_for_each(array, axis):
    devices = lax.axis_size(axis)
    return lax.all_to_all(
        jnp.broadcast_to(array[None], (devices, *array.shape)), axis, 0, 0, tiled=True
    )


def of_everyone(array, axis):
    everything = copy_for_each(array, axis)
    return jnp.sum(everything, axis=0)


def in_one(arrays, axis):
    ends = [0]
    for a in arrays:
        ends.append(ends[-1] + a.size)
    subtotal = of_everyone(jnp.concatenate([a.ravel() for a in arrays]), axis)
    return tuple((subtotal[b:e].reshape(a.shape) for a, b, e in zip(arrays, ends, ends[1:])))


def in_one_piece(arrays, axis, dim, along):
    ends, at = ([], 0)
    for a in arrays[:-1]:
        at += a.shape[along]
        ends.append(at)
    both = jnp.concatenate(arrays, axis=along)
    return tuple(jnp.split(lax.all_gather(both, axis, axis=dim, tiled=True), ends, axis=along))


def laid_out(pieces, dim):
    pieces = jnp.moveaxis(pieces, 0, dim)
    shape = pieces.shape
    return pieces.reshape(*shape[:dim], shape[dim] * shape[dim + 1], *shape[dim + 2 :])


def gather_in_order(array, axes, order):
    pieces = array[None]
    for k in order:
        pieces = lax.all_gather(pieces, axes[k], axis=0, tiled=True)
    carried = [lax.axis_size(axes[k]) for k in reversed(order)]
    pieces = pieces.reshape(*carried, *array.shape)
    turned = sorted(range(len(order)), key=lambda place: order[len(order) - 1 - place])
    return pieces.transpose(*turned, *range(len(order), pieces.ndim)).reshape(-1, *array.shape)


def gather_axes(array, axes, order, dim):
    return laid_out(gather_in_order(array, axes, order), dim)


def per_device(
    one_query,
    other_query,
    one_key,
    other_key,
    one_value,
    other_value,
    mix_share,
    norm_train,
    norm_step,
):
    result_query = mix_share[:, None] * one_query + (1.0 - mix_share[:, None]) * other_query
    result_key = mix_share[:, None] * one_key + (1.0 - mix_share[:, None]) * other_key
    result_value = mix_share[:, None] * one_value + (1.0 - mix_share[:, None]) * other_value
    total_query, total_key, total_value = in_one(
        (
            jnp.sum(result_query * result_query, axis=0),
            jnp.sum(result_key * result_key, axis=0),
            jnp.sum(result_value * result_value, axis=0),
        ),
        FSDP,
    )
    scale_query = jnp.sqrt(total_query)
    scale_key = jnp.sqrt(total_key)
    scale_value = jnp.sqrt(total_value)
    narrow_query, narrow_key, narrow_value = (
        (result_query / scale_query).astype(jnp.bfloat16),
        (result_key / scale_key).astype(jnp.bfloat16),
        (result_value / scale_value).astype(jnp.bfloat16),
    )
    final_query, final_key, final_value = in_one_piece(
        (narrow_query, narrow_key, narrow_value), FSDP, 0, 1
    )
    serve_norm = gather_axes(
        (norm_train + norm_step).astype(jnp.bfloat16), FSDP_COLS, (0, 2, 3, 1), 0
    )
    return (final_query, final_key, final_value, scale_query, scale_key, scale_value, serve_norm)


def solution(mesh):
    split = Mesh(mesh.devices.reshape(8, 2, 4, 4), ("fsdp_0", "fsdp_1", "cols_0", "cols_1"))
    placed = (
        P(FSDP, COLS),
        P(FSDP, COLS),
        P(FSDP, COLS),
        P(FSDP, COLS),
        P(FSDP, COLS),
        P(FSDP, COLS),
        P(FSDP),
        P(FSDP_COLS),
        P(FSDP_COLS),
    )
    return jax.shard_map(
        per_device,
        mesh=split,
        in_specs=placed,
        out_specs=(P(None, COLS), P(None, COLS), P(None, COLS), P(COLS), P(COLS), P(COLS), P()),
        check_vma=False,
    )
```

profile of v0, /device:TPU:1, one launch (start us, length us, event | category | flops | bytes accessed | tf_op | source)
XLA Modules:
  0.0 84.9 jit_solution(10052405259920044924)
XLA Ops:
  7.2 0.0 all-gather.4.cloned.1.call-start
  7.2 0.7 broadcast_subtract_fusion
  7.9 0.0 copy-start.5
  7.9 0.0 copy-start.3
  7.9 0.0 copy-start.4
  7.9 1.6 %multiply_reduce_fusion.2 = (f32[256]{0:T(256)S(1)}, f32[256]{0:T(256)S(1)}, f32[256]{0:T(256)S(1)}) fusion(f32[256,256]{1,0:T(8,128)} %param.10, f32[256]{0:T(256)S(1)} %broadcast_subtract_fusion, f32[256,256]{1,0:T(8,128)} %param.9, f32[256]{0:T(256)} %param.15, f32[256,256]{1,0:T(8,128)} %param.12, f32[256,256]{1,0:T(8,128)} %param.11, ...), kind=kLoop, calls=%fused_computation.8 | loop fusion | flops 982272 | bytes 1577984 | tf_op jit(solution)/shard_map/reduce_sum | solution.py:77
  9.6 17.2 %all_to_all.6 = f32[16,1,768]{2,1,0:T(1,128)S(1)} all-to-all(f32[16,1,768]{2,1,0:T(1,128)S(1)} %broadcast_in_dim.4), channel_id=1, replica_groups=mesh['fsdp_0'=8,'fsdp_1'=2,'cols_0'=4,'cols_1'=4] {'fsdp_0','fsdp_1'}, dimensions={0} | all-to-all | bytes 98304 | tf_op jit(solution)/shard_map/all_to_all | solution.py:14
  26.9 0.0 copy-start
  26.9 0.0 copy-start.1
  26.9 0.0 copy-start.2
  26.9 1.6 %divide_convert_fusion.2 = (bf16[256,256]{1,0:T(8,128)(2,1)S(1)}, bf16[256,256]{1,0:T(8,128)(2,1)S(1)}, bf16[256,256]{1,0:T(8,128)(2,1)S(1)}) fusion(f32[256]{0:T(256)S(1)} %get-tuple-element.13, f32[256,256]{1,0:T(8,128)} %param.10, f32[256]{0:T(256)S(1)} %broadcast_subtract_fusion, f32[256,256]{1,0:T(8,128)} %param.9, f32[256]{0:T(256)} %param.15, ...), kind=kLoop, calls=%fused_computation.3 | loop fusion | flops 983040 | bytes 1971200 | tf_op jit(solution)/shard_map/convert_element_type | solution.py:87
  28.5 0.8 pad_maximum_fusion
  29.2 0.0 all-gather.4.cloned.1.call-update
  29.3 0.0 copy-done.5
  29.3 0.6 dynamic-slice
  30.5 0.0 copy-done.3
  30.5 0.0 copy-done.4
  30.6 0.2 dynamic-update-slice
  30.8 11.3 %all-reduce = bf16[128]{0:T(256)(128)(2,1)S(1)} all-reduce(bf16[128]{0:T(256)(128)(2,1)S(1)} %dynamic-update-slice), channel_id=2, replica_groups=mesh['fsdp_0'=8,'fsdp_1'=2,'cols_0'=4,'cols_1'=4] {'fsdp_0'}, use_global_device_ids=true, to_apply=%add | all-reduce | flops 128 | bytes 512
  42.1 0.1 reshape.30
  42.2 10.2 %all_gather.17 = bf16[32,16]{1,0:T(8,128)(2,1)S(1)} all-gather(bf16[8,16]{1,0:T(8,128)(2,1)S(1)} %reshape.30), channel_id=1, replica_groups=mesh['fsdp_0'=8,'fsdp_1'=2,'cols_0'=4,'cols_1'=4] {'cols_0'}, dimensions={0}, use_global_device_ids=true | all-gather | bytes 1280 | tf_op jit(solution)/shard_map/all_gather | solution.py:50
  52.4 0.1 copy.24
  52.5 10.4 %all-gather.1 = bf16[4,32,16]{1,2,0:T(8,128)(2,1)S(1)} all-gather(bf16[1,32,16]{1,2,0:T(8,128)(2,1)S(1)} %copy.24), channel_id=1, replica_groups=mesh['fsdp_0'=8,'fsdp_1'=2,'cols_0'=4,'cols_1'=4] {'cols_1'}, dimensions={0}, use_global_device_ids=true | all-gather | bytes 5120 | tf_op jit(solution)/shard_map/all_gather | solution.py:50
  62.9 0.1 copy.25
  63.0 8.5 %all_gather.19 = bf16[256,16]{1,0:T(8,128)(2,1)S(1)} all-gather(bf16[128,16]{1,0:T(8,128)(2,1)S(1)} %bitcast.7), channel_id=1, replica_groups=mesh['fsdp_0'=8,'fsdp_1'=2,'cols_0'=4,'cols_1'=4] {'fsdp_1'}, dimensions={0}, use_global_device_ids=true | all-gather | bytes 12288 | tf_op jit(solution)/shard_map/all_gather | solution.py:50
  71.5 0.7 reshape_reshape.3
  72.2 0.1 all-gather.4.cloned.1.call-done
  72.3 5.7 %fusion = (bf16[4096,256]{1,0:T(8,128)(2,1)}, bf16[4096,256]{1,0:T(8,128)(2,1)}, bf16[4096,256]{1,0:T(8,128)(2,1)}) fusion(bf16[4096,768]{1,0:T(8,128)(2,1)} %all-gather.4.cloned.1.call-done), kind=kLoop, calls=%fused_computation.16 | loop fusion | bytes 12582912 | tf_op jit(solution)/shard_map/split | solution.py:38
  78.0 0.0 copy-done
  78.0 0.0 copy-done.1
  78.0 0.0 copy-done.2
  (7 shorter events, 0.1 us)
Async XLA Ops:
  7.2 65.1 %all-gather.4.cloned.1.call-start = ((), (), s32[]{:S(2)}) async-start(), calls=%async_computation.1 | async-start | bytes 6684672 | tf_op jit(solution)/shard_map/all_gather | solution.py:38
  7.9 21.4 %copy-start.5 = (u32[256]{0:T(256)S(1)}, u32[256]{0:T(256)}, u32[]{:S(2)}) copy-start(u32[256]{0:T(256)} %constant.8) | copy-start | bytes 3076
  7.9 22.6 %copy-start.3 = (f32[16]{0:T(128)S(1)}, f32[16]{0:T(128)}, u32[]{:S(2)}) copy-start(f32[16]{0:T(128)} %param.16) | copy-start | bytes 196
  7.9 22.6 %copy-start.4 = (f32[16]{0:T(128)S(1)}, f32[16]{0:T(128)}, u32[]{:S(2)}) copy-start(f32[16]{0:T(128)} %param.17) | copy-start | bytes 196
  26.9 51.2 %copy-start = (f32[256]{0:T(256)}, f32[256]{0:T(256)S(1)}, u32[]{:S(2)}) copy-start(f32[256]{0:T(256)S(1)} %get-tuple-element.13) | copy-start | bytes 3076
  26.9 51.2 %copy-start.1 = (f32[256]{0:T(256)}, f32[256]{0:T(256)S(1)}, u32[]{:S(2)}) copy-start(f32[256]{0:T(256)S(1)} %get-tuple-element.14) | copy-start | bytes 3076
  26.9 51.1 %copy-start.2 = (f32[256]{0:T(256)}, f32[256]{0:T(256)S(1)}, u32[]{:S(2)}) copy-start(f32[256]{0:T(256)S(1)} %get-tuple-element.15) | copy-start | bytes 3076
Sparse Core Ops, SparseCore 0:
  29.4 42.8 all-gather.3
where the time goes:
time: 85.1 us; the launch traced here: 84.9 us
  blocking collectives  57.7 us (68%)
  between operations  14.8 us (17%)
  local copies, waits for them, and re-layouts  7.63 us (9%)
  other arithmetic  4.67 us (5%)
    all_gather x3, blocking collectives, gather_in_order(): pieces = lax.all_gather(pieces, axes[k], axis=0, tiled=True)  29.1 us
    all_to_all x1, blocking collectives, copy_for_each(): lax.all_to_all(jnp.broadcast_to(array[None], (devices, *array.shape)), ax...  17.2 us
    unnamed x1, blocking collectives  11.3 us
    split x1, local copies, waits for them, and re-layouts, in_one_piece(): jnp.split(lax.all_gather(both, axis, axis=dim, tiled=True), ends, axis=al...  5.72 us
  transfers between devices with their start and end apart: 1, of which 1 were waited for; matrix products, arithmetic and copies ran while one was open for 2% of the time, Pallas kernels for 0%

commit v1 on v0

v1 whole, which is shorter than its diff:
```python
import functools

import jax
import jax.numpy as jnp
from jax import lax
from jax.experimental import pallas as pl
from jax.experimental.pallas import tpu as pltpu
from jax.sharding import Mesh
from jax.sharding import PartitionSpec as P

FSDP = ("fsdp_0", "fsdp_1")
FSDP_COLS = ("fsdp_0", "fsdp_1", "cols_0", "cols_1")
COLS = ("cols_0", "cols_1")
MESH = pl.DeviceIdType.MESH

Z = 8
CORES = 2
SHARDS = Z * CORES
PLANE_Y = 4
PLANE_X = 4
PLANE = PLANE_Y * PLANE_X
ROWS = 256
HALF = 128
LANES = 128
PIECE = 16
NEAR = [(d, a, h) for d in (1, 2, 3) for a in range(3) for h in range(2)]
STREAM = (
    NEAR + [(4, a, 0) for a in range(3)],
    NEAR + [(4, a, 1) for a in range(3)],
)
STEPS = len(STREAM[0])


def kernel(
    oq, tq, ok, tk, ov, tv, share, train, step,
    out_q, out_k, out_v, scale_q, scale_k, scale_v, norm,
    ins, share_v, norm_in, mixed, msg, sums, plane_out, plane_in, norm_f32,
    in_sem, sum_send, sum_recv, plane_send, plane_recv,
    ici_send, ici_recv, own_send, own_recv, d2d_send, d2d_recv,
):
    z, c = lax.axis_index("fsdp_0"), lax.axis_index("fsdp_1")
    col = lax.axis_index("cols_0") * PLANE_X + lax.axis_index("cols_1")
    me = z * CORES + c
    outs = (out_q, out_k, out_v)

    def fsdp_peers():
        for dz in (4, 5, 3, 6, 2, 7, 1, 0):
            for dc in (0, 1):
                if dz or dc:
                    pz, pc = lax.rem(z + dz, Z), lax.rem(c + dc, CORES)
                    yield {"fsdp_0": pz, "fsdp_1": pc}, pz * CORES + pc

    def plane_peers():
        for k in range(1, PLANE):
            p = lax.rem(col + k, PLANE)
            yield {"cols_0": p // PLANE_X, "cols_1": lax.rem(p, PLANE_X)}, p

    barrier = pltpu.get_barrier_semaphore()
    for device, _ in list(fsdp_peers()) + list(plane_peers()):
        pl.semaphore_signal(barrier, inc=1, device_id=device, device_id_type=MESH)

    loads = [pltpu.make_async_copy(share, share_v, in_sem.at[6])]
    loads += [
        pltpu.make_async_copy(src, ins.at[i], in_sem.at[i])
        for i, src in enumerate((oq, tq, ok, tk, ov, tv))
    ]
    loads += [
        pltpu.make_async_copy(train, norm_in.at[0], in_sem.at[7]),
        pltpu.make_async_copy(step, norm_in.at[1], in_sem.at[8]),
    ]
    for load in loads:
        load.start()

    msg[...] = jnp.zeros_like(msg)
    loads[0].wait()
    shares = [
        jnp.broadcast_to(share_v[:, r * HALF : (r + 1) * HALF], (LANES, HALF)).T for r in range(2)
    ]
    for a in range(3):
        loads[1 + 2 * a].wait()
        loads[2 + 2 * a].wait()
        for j in range(2):
            lanes = pl.ds(j * LANES, LANES)
            total = jnp.zeros((1, LANES), jnp.float32)
            for r in range(2):
                rows = pl.ds(r * HALF, HALF)
                value = shares[r] * ins[2 * a, rows, lanes] + (1.0 - shares[r]) * ins[2 * a + 1, rows, lanes]
                mixed[a, rows, lanes] = value
                total = total + jnp.sum(value * value, axis=0, keepdims=True)
            msg[pl.ds(2 * a + j, 1), :] = total
    loads[7].wait()
    loads[8].wait()
    piece = jnp.concatenate(
        [norm_in[0] + norm_in[1], jnp.zeros((1, LANES - PIECE), jnp.float32)], axis=1
    )
    piece = pltpu.roll(jnp.broadcast_to(piece, (8, LANES)), lax.rem(col, 8) * PIECE, 1)
    msg[pl.ds(6, 1), :] = piece[:1]

    pl.semaphore_wait(barrier, SHARDS - 1 + PLANE - 1)

    exchanges = []
    for device, p in fsdp_peers():
        copy = pltpu.make_async_remote_copy(
            src_ref=msg, dst_ref=sums.at[me], send_sem=sum_send.at[p], recv_sem=sum_recv.at[me],
            device_id=device, device_id_type=MESH,
        )
        copy.start()
        exchanges.append(copy)
    sums[pl.ds(me, 1)] = msg[...][None]
    arrivals = []
    for device, p in fsdp_peers():
        arrivals.append(pltpu.make_async_remote_copy(
            src_ref=msg, dst_ref=sums.at[p], send_sem=sum_send.at[p], recv_sem=sum_recv.at[p],
            device_id=device, device_id_type=MESH,
        ))
    for copy in arrivals:
        copy.wait_recv()

    total = sums[0]
    for s in range(1, SHARDS):
        total = total + sums[s]
    scale = jnp.sqrt(total)
    inverse = 1.0 / scale
    own = pl.multiple_of(me * ROWS, ROWS)
    for a, out in enumerate(outs):
        for r in range(2):
            for j in range(2):
                lanes = pl.ds(j * LANES, LANES)
                value = mixed[a, pl.ds(r * HALF, HALF), lanes] * inverse[2 * a + j : 2 * a + j + 1]
                out[pl.ds(pl.multiple_of(own + r * HALF, HALF), HALF), lanes] = value.astype(jnp.bfloat16)

    def chunk(shard, a, h):
        return outs[a].at[pl.ds(pl.multiple_of(shard * ROWS + h * HALF, HALF), HALF)]

    def along(way, i):
        d, a, h = STREAM[way][i]
        source = lax.rem(z + (Z - d if way == 0 else d), Z)
        return source * CORES + c, a, h

    def hop(way, i, shard, a, h):
        ref = chunk(shard, a, h)
        target = lax.rem(z + (1 if way == 0 else Z - 1), Z)
        return pltpu.make_async_remote_copy(
            src_ref=ref, dst_ref=ref, send_sem=ici_send.at[way, i], recv_sem=ici_recv.at[way, i],
            device_id={"fsdp_0": target}, device_id_type=MESH,
        )

    def across(send, recv, shard, a, h):
        ref = chunk(shard, a, h)
        return pltpu.make_async_remote_copy(
            src_ref=ref, dst_ref=ref, send_sem=send, recv_sem=recv,
            device_id={"fsdp_1": 1 - c}, device_id_type=MESH,
        )

    sent = list(exchanges)
    for a in range(3):
        for h in range(2):
            for way in range(2):
                copy = hop(way, 2 * a + h, me, a, h)
                copy.start()
                sent.append(copy)
    for a in range(3):
        for h in range(2):
            copy = across(own_send.at[2 * a + h], own_recv.at[2 * a + h], me, a, h)
            copy.start()
            sent.append(copy)

    for a, ref in enumerate((scale_q, scale_k, scale_v)):
        for j in range(2):
            ref[:, pl.ds(j * LANES, LANES)] = scale[2 * a + j : 2 * a + j + 1]

    for s in range(SHARDS):
        plane_out[pl.ds(s, 1), :] = sums[s, 6:7, :]
    for device, p in plane_peers():
        copy = pltpu.make_async_remote_copy(
            src_ref=plane_out, dst_ref=plane_in.at[col], send_sem=plane_send.at[p], recv_sem=plane_recv.at[col],
            device_id=device, device_id_type=MESH,
        )
        copy.start()
        sent.append(copy)
    plane_in[pl.ds(col, 1)] = plane_out[...][None]

    for i in range(STEPS):
        for way in range(2):
            d, a, h = STREAM[way][i]
            shard, _, _ = along(way, i)
            hop(way, i, shard, a, h).wait_recv()
            if (d + 1, a, h) in STREAM[way]:
                copy = hop(way, STREAM[way].index((d + 1, a, h)), shard, a, h)
                copy.start()
                sent.append(copy)
            copy = across(d2d_send.at[way, i], d2d_recv.at[way, i], shard, a, h)
            copy.start()
            sent.append(copy)

    for device, p in plane_peers():
        pltpu.make_async_remote_copy(
            src_ref=plane_out, dst_ref=plane_in.at[p], send_sem=plane_send.at[p], recv_sem=plane_recv.at[p],
            device_id=device, device_id_type=MESH,
        ).wait_recv()
    for side in range(2):
        gathered = plane_in[8 * side]
        for k in range(1, 8):
            gathered = gathered + plane_in[8 * side + k]
        norm_f32[pl.ds(side, SHARDS, stride=2), :] = gathered
    norm[...] = norm_f32[...].astype(jnp.bfloat16)

    partner = z * CORES + 1 - c
    for a in range(3):
        for h in range(2):
            across(own_send.at[2 * a + h], own_recv.at[2 * a + h], partner, a, h).wait_recv()
    for i in range(STEPS):
        for way in range(2):
            shard, a, h = along(way, i)
            across(d2d_send.at[way, i], d2d_recv.at[way, i], shard + 1 - 2 * c, a, h).wait_recv()
    for copy in sent:
        copy.wait_send()


def per_device(oq, tq, ok, tk, ov, tv, share, train, step):
    f32, bf16 = jnp.float32, jnp.bfloat16
    whole = jax.ShapeDtypeStruct((SHARDS * ROWS, 2 * LANES), bf16)
    scale = jax.ShapeDtypeStruct((1, 2 * LANES), f32)
    vmem = pl.BlockSpec(memory_space=pltpu.VMEM)
    dma = pltpu.SemaphoreType.DMA
    outs = pl.pallas_call(
        kernel,
        name="mix_and_gather",
        out_shape=(whole, whole, whole, scale, scale, scale, jax.ShapeDtypeStruct((32, LANES), bf16)),
        in_specs=[pl.BlockSpec(memory_space=pl.ANY)] * 9,
        out_specs=(vmem,) * 7,
        scratch_shapes=[
            pltpu.VMEM((6, ROWS, 2 * LANES), f32),
            pltpu.VMEM((1, ROWS), f32),
            pltpu.VMEM((2, 1, PIECE), f32),
            pltpu.VMEM((3, ROWS, 2 * LANES), f32),
            pltpu.VMEM((8, LANES), f32),
            pltpu.VMEM((SHARDS, 8, LANES), f32),
            pltpu.VMEM((SHARDS, LANES), f32),
            pltpu.VMEM((PLANE, SHARDS, LANES), f32),
            pltpu.VMEM((32, LANES), f32),
            dma((9,)),
            dma((SHARDS,)),
            dma((SHARDS,)),
            dma((PLANE,)),
            dma((PLANE,)),
            dma((2, STEPS)),
            dma((2, STEPS)),
            dma((6,)),
            dma((6,)),
            dma((2, STEPS)),
            dma((2, STEPS)),
        ],
        compiler_params=pltpu.CompilerParams(collective_id=0, has_side_effects=True),
    )(oq, tq, ok, tk, ov, tv, share.reshape(1, -1), train.reshape(1, -1), step.reshape(1, -1))
    q, k, v, scale_q, scale_k, scale_v, norm = outs
    return q, k, v, scale_q.reshape(-1), scale_k.reshape(-1), scale_v.reshape(-1), norm.reshape(-1)


def solution(mesh):
    split = Mesh(mesh.devices.reshape(Z, CORES, PLANE_Y, PLANE_X), FSDP_COLS)
    block = P(FSDP, COLS)
    return jax.shard_map(
        per_device,
        mesh=split,
        in_specs=(block,) * 6 + (P(FSDP), P(FSDP_COLS), P(FSDP_COLS)),
        out_specs=(P(None, COLS),) * 3 + (P(COLS),) * 3 + (P(),),
        check_vma=False,
    )
```

time: 85.1 us -> 63.7 us (0.75)
  blocking collectives: 57.7 us -> 0 us
  Pallas kernels: 0 us -> 53.8 us
  between operations: 14.8 us -> 0.66 us
  other arithmetic: 4.67 us -> 0 us
  local copies, waits for them, and re-layouts: 7.63 us -> 9.17 us
    pallas_call x0 -> x1, Pallas kernels: none -> 53.8 us  [per_device(): pl.pallas_call(kernel, name='mix_and_gather', out_shape=(whole, whole, wh...]
    all_gather x3 -> x0, blocking collectives: 29.1 us -> none  [gather_in_order(): pieces = lax.all_gather(pieces, axes[k], axis=0, tiled=True)]
    all_to_all x1 -> x0, blocking collectives: 17.2 us -> none  [copy_for_each(): lax.all_to_all(jnp.broadcast_to(array[None], (devices, *array.shape)), ax...]
    unnamed x1 -> x0, blocking collectives: 11.3 us -> none
    unnamed x16 -> x19, local copies, waits for them, and re-layouts: 0.94 us -> 9.17 us
    split x1 -> x0, local copies, waits for them, and re-layouts: 5.72 us -> none  [in_one_piece(): jnp.split(lax.all_gather(both, axis, axis=dim, tiled=True), ends, axis=al...]
    reduce_sum x2 -> x0, other arithmetic: 1.65 us -> none  [the longest x1 1.6 us: per_device(): jnp.sum(result_query * result_query, axis=0)]
    convert_element_type x2 -> x0, other arithmetic: 1.56 us -> none  [the longest x1 1.55 us: per_device(): (result_query / scale_query).astype(jnp.bfloat16)]
  transfers between devices with their start and end apart: 1 -> 0, of which waited for: 1 -> 0; matrix products, arithmetic and copies ran while one was open for 2% -> 0% of each run, Pallas kernels for 0% -> 0%
where the time goes in v1:
time: 63.7 us; the launch traced here: 63.6 us
  Pallas kernels  53.8 us (84%)
  local copies, waits for them, and re-layouts  9.17 us (14%)
  between operations  0.66 us (1%)
    pallas_call x1, Pallas kernels, per_device(): pl.pallas_call(kernel, name='mix_and_gather', out_shape=(whole, whole, wh...  53.8 us
    unnamed x19, local copies, waits for them, and re-layouts  9.17 us

profile of v1, /device:TPU:1, one launch (start us, length us, event | category | flops | bytes accessed | tf_op | source)
XLA Modules:
  0.0 63.6 jit_solution(2770060283500968283)
XLA Ops:
  0.6 53.8 %mix_and_gather.1 = (bf16[4096,256]{1,0:T(8,128)(2,1)}, bf16[4096,256]{1,0:T(8,128)(2,1)}, bf16[4096,256]{1,0:T(8,128)(2,1)}, f32[1,256]{1,0:T(1,128)}, f32[1,25...) custom-call(f32[256,256]{1,0:T(8,128)} %oq.1, f32[256,256]{1,0:T(8,128)} %tq.1, f32[256,256]{1,0:T(8,128)} %ok.1, ...), custom_call_target="tpu_custom_call" | custom-call | tf_op jit(solution)/shard_map/mix_and_gather/pallas_call | solution.py:226
  54.4 0.0 copy-start.1
  54.4 3.2 %copy.23 = bf16[4096,256]{1,0:T(8,128)(2,1)} copy(bf16[4096,256]{1,0:T(8,128)(2,1)} %get-tuple-element.28) | data formatting | bytes 4194304
  57.6 0.0 copy-done.1
  57.6 0.0 copy-start
  57.6 1.3 %copy.24 = bf16[4096,256]{1,0:T(8,128)(2,1)} copy(bf16[4096,256]{1,0:T(8,128)(2,1)S(1)} %copy-done.1) | data formatting | bytes 4194304
  58.9 1.0 %copy-done = bf16[4096,256]{1,0:T(8,128)(2,1)S(1)} copy-done((bf16[4096,256]{1,0:T(8,128)(2,1)S(1)}, bf16[4096,256]{1,0:T(8,128)(2,1)}, u32[]{:S(2)}) %copy-start) | copy-done | bytes 2097176
  60.0 0.0 copy-start.5
  60.0 0.0 copy-start.4
  60.0 0.0 copy-start.3
  60.0 0.0 copy-start.2
  60.0 1.3 %copy.25 = bf16[4096,256]{1,0:T(8,128)(2,1)} copy(bf16[4096,256]{1,0:T(8,128)(2,1)S(1)} %copy-done) | data formatting | bytes 4194304
  61.3 0.0 copy-done.5
  61.3 0.6 copy.26
  61.9 0.0 copy-done.4
  61.9 0.6 copy.27
  62.4 0.0 copy-done.3
  62.4 0.6 copy.28
  63.0 0.0 copy-done.2
  63.0 0.6 copy.29
Async XLA Ops:
  54.4 3.2 %copy-start.1 = (bf16[4096,256]{1,0:T(8,128)(2,1)S(1)}, bf16[4096,256]{1,0:T(8,128)(2,1)}, u32[]{:S(2)}) copy-start(bf16[4096,256]{1,0:T(8,128)(2,1)} %get-tuple-element.29) | copy-start | bytes 6291460
  57.6 2.3 %copy-start = (bf16[4096,256]{1,0:T(8,128)(2,1)S(1)}, bf16[4096,256]{1,0:T(8,128)(2,1)}, u32[]{:S(2)}) copy-start(bf16[4096,256]{1,0:T(8,128)(2,1)} %get-tuple-element.30) | copy-start | bytes 6291460
  60.0 1.3 %copy-start.5 = (f32[1,256]{1,0:T(1,128)S(1)}, f32[1,256]{1,0:T(1,128)}, u32[]{:S(2)}) copy-start(f32[1,256]{1,0:T(1,128)} %get-tuple-element.17) | copy-start | bytes 3076
  60.0 1.9 %copy-start.4 = (f32[1,256]{1,0:T(1,128)S(1)}, f32[1,256]{1,0:T(1,128)}, u32[]{:S(2)}) copy-start(f32[1,256]{1,0:T(1,128)} %get-tuple-element.18) | copy-start | bytes 3076
  60.0 2.5 %copy-start.3 = (f32[1,256]{1,0:T(1,128)S(1)}, f32[1,256]{1,0:T(1,128)}, u32[]{:S(2)}) copy-start(f32[1,256]{1,0:T(1,128)} %get-tuple-element.19) | copy-start | bytes 3076
  60.0 3.0 %copy-start.2 = (bf16[32,128]{1,0:T(8,128)(2,1)S(1)}, bf16[32,128]{1,0:T(8,128)(2,1)}, u32[]{:S(2)}) copy-start(bf16[32,128]{1,0:T(8,128)(2,1)} %get-tuple-element.20) | copy-start | bytes 24580

commit v2 on v1

--- a/solution.py
+++ b/solution.py
@@ -217,6 +217,36 @@
         copy.wait_send()
 
 
+PARTS = 4
+
+
+def store_kernel(*refs):
+    ins, outs, sem = refs[:7], refs[7:14], refs[14]
+    copies = []
+    for i, (src, dst) in enumerate(zip(ins, outs)):
+        parts = PARTS if i < 3 else 1
+        rows = src.shape[0] // parts
+        for p in range(parts):
+            window = pl.ds(p * rows, rows)
+            copies.append(pltpu.make_async_copy(src.at[window], dst.at[window], sem.at[len(copies)]))
+    for copy in copies:
+        copy.start()
+    for copy in copies:
+        copy.wait()
+
+
+def store(arrays):
+    return pl.pallas_call(
+        store_kernel,
+        name="store",
+        out_shape=tuple(jax.ShapeDtypeStruct(a.shape, a.dtype) for a in arrays),
+        in_specs=[pl.BlockSpec(memory_space=pltpu.VMEM)] * 7,
+        out_specs=(pl.BlockSpec(memory_space=pltpu.HBM),) * 7,
+        scratch_shapes=[pltpu.SemaphoreType.DMA((3 * PARTS + 4,))],
+        compiler_params=pltpu.CompilerParams(vmem_limit_bytes=16 * 2**20),
+    )(*arrays)
+
+
 def per_device(oq, tq, ok, tk, ov, tv, share, train, step):
     f32, bf16 = jnp.float32, jnp.bfloat16
     whole = jax.ShapeDtypeStruct((SHARDS * ROWS, 2 * LANES), bf16)
@@ -227,7 +257,7 @@
         kernel,
         name="mix_and_gather",
         out_shape=(whole, whole, whole, scale, scale, scale, jax.ShapeDtypeStruct((32, LANES), bf16)),
-        in_specs=[pl.BlockSpec(memory_space=pl.ANY)] * 9,
+        in_specs=[pl.BlockSpec(memory_space=pltpu.HBM)] * 9,
         out_specs=(vmem,) * 7,
         scratch_shapes=[
             pltpu.VMEM((6, ROWS, 2 * LANES), f32),
@@ -251,9 +281,11 @@
             dma((2, STEPS)),
             dma((2, STEPS)),
         ],
-        compiler_params=pltpu.CompilerParams(collective_id=0, has_side_effects=True),
-    )(oq, tq, ok, tk, ov, tv, share.reshape(1, -1), train.reshape(1, -1), step.reshape(1, -1))
-    q, k, v, scale_q, scale_k, scale_v, norm = outs
+        compiler_params=pltpu.CompilerParams(collective_id=0, has_side_effects=True, vmem_limit_bytes=24 * 2**20),
+    )(*(pltpu.with_memory_space_constraint(a, pltpu.HBM) for a in (
+        oq, tq, ok, tk, ov, tv, share.reshape(1, -1), train.reshape(1, -1), step.reshape(1, -1)
+    )))
+    q, k, v, scale_q, scale_k, scale_v, norm = store(outs)
     return q, k, v, scale_q.reshape(-1), scale_k.reshape(-1), scale_v.reshape(-1), norm.reshape(-1)
 
 

time: 63.7 us -> 54.7 us (0.86)
  local copies, waits for them, and re-layouts: 9.17 us -> 0 us
    unnamed x19 -> x0, local copies, waits for them, and re-layouts: 9.17 us -> none
    pallas_call x0 -> x1, Pallas kernels: none -> 2.8 us  [store(): pl.pallas_call(store_kernel, name='store', out_shape=tuple((jax.ShapeDtyp...]
    pallas_call x1, Pallas kernels: 53.8 us -> 51.2 us  [per_device(): pl.pallas_call(kernel, name='mix_and_gather', out_shape=(whole, whole, wh...]
where the time goes in v2:
time: 54.7 us; the launch traced here: 54.6 us
  Pallas kernels  54 us (99%)
  between operations  0.64 us (1%)
    pallas_call x1, Pallas kernels, per_device(): pl.pallas_call(kernel, name='mix_and_gather', out_shape=(whole, whole, wh...  51.2 us
    pallas_call x1, Pallas kernels, store(): pl.pallas_call(store_kernel, name='store', out_shape=tuple((jax.ShapeDtyp...  2.8 us

profile of v2, /device:TPU:1, one launch (start us, length us, event | category | flops | bytes accessed | tf_op | source)
XLA Modules:
  0.0 54.6 jit_solution(2284975482504824483)
XLA Ops:
  0.6 51.2 %mix_and_gather.1 = (bf16[4096,256]{1,0:T(8,128)(2,1)S(1)}, bf16[4096,256]{1,0:T(8,128)(2,1)S(1)}, bf16[4096,256]{1,0:T(8,128)(2,1)S(1)}, f32[1,256]{1,0:T(1,128...) custom-call(f32[256,256]{1,0:T(8,128)} %oq.1, f32[256,256]{1,0:T(8,128)} %tq.1, ...), custom_call_target="tpu_custom_call" | custom-call | tf_op jit(solution)/shard_map/mix_and_gather/pallas_call | solution.py:256
  51.8 2.8 %store.1 = (bf16[4096,256]{1,0:T(8,128)(2,1)}, bf16[4096,256]{1,0:T(8,128)(2,1)}, bf16[4096,256]{1,0:T(8,128)(2,1)}, f32[1,256]{1,0:T(1,128)}, f32[1,256]{1,0:T(...) custom-call(bf16[4096,256]{1,0:T(8,128)(2,1)S(1)} %get-tuple-element.21.refs_0_, ...), custom_call_target="tpu_custom_call" | custom-call | tf_op jit(solution)/shard_map/store/pallas_call | solution.py:239

commit v3 on v2

--- a/solution.py
+++ b/solution.py
@@ -29,13 +29,15 @@
     NEAR + [(4, a, 1) for a in range(3)],
 )
 STEPS = len(STREAM[0])
+EARLY = [(0, 0), (0, 1)]
+ANSWER = 8
 
 
 def kernel(
     oq, tq, ok, tk, ov, tv, share, train, step,
     out_q, out_k, out_v, scale_q, scale_k, scale_v, norm,
-    ins, share_v, norm_in, mixed, msg, sums, plane_out, plane_in, norm_f32,
-    in_sem, sum_send, sum_recv, plane_send, plane_recv,
+    ins, share_v, norm_in, mixed, landed, msg, sums, plane_out, plane_in, norm_f32,
+    in_sem, sum_send, sum_recv, plane_send, plane_recv, answer_send, answer_recv,
     ici_send, ici_recv, own_send, own_recv, d2d_send, d2d_recv,
 ):
     z, c = lax.axis_index("fsdp_0"), lax.axis_index("fsdp_1")
@@ -51,13 +53,50 @@
                     yield {"fsdp_0": pz, "fsdp_1": pc}, pz * CORES + pc
 
     def plane_peers():
-        for k in range(1, PLANE):
-            p = lax.rem(col + k, PLANE)
-            yield {"cols_0": p // PLANE_X, "cols_1": lax.rem(p, PLANE_X)}, p
+        for p in range(1, PLANE):
+            yield {"cols_0": p // PLANE_X, "cols_1": p % PLANE_X}, p
 
     barrier = pltpu.get_barrier_semaphore()
-    for device, _ in list(fsdp_peers()) + list(plane_peers()):
+    for device, _ in fsdp_peers():
         pl.semaphore_signal(barrier, inc=1, device_id=device, device_id_type=MESH)
+
+    @pl.when(col == 0)
+    def _():
+        for device, _ in plane_peers():
+            pl.semaphore_signal(barrier, inc=1, device_id=device, device_id_type=MESH)
+
+    def chunk(shard, a, h):
+        return outs[a].at[pl.ds(pl.multiple_of(shard * ROWS + h * HALF, HALF), HALF)]
+
+    def along(way, i):
+        d, a, h = STREAM[way][i]
+        source = lax.rem(z + (Z - d if way == 0 else d), Z)
+        return source * CORES + c, a, h
+
+    def hop(way, i, shard, a, h):
+        ref = chunk(shard, a, h)
+        target = lax.rem(z + (1 if way == 0 else Z - 1), Z)
+        return pltpu.make_async_remote_copy(
+            src_ref=ref, dst_ref=ref, send_sem=ici_send.at[way, i], recv_sem=ici_recv.at[way, i],
+            device_id={"fsdp_0": target}, device_id_type=MESH,
+        )
+
+    def early(way, e):
+        a, h = EARLY[e]
+        i = STREAM[way].index((1, a, h))
+        target = lax.rem(z + (1 if way == 0 else Z - 1), Z)
+        return pltpu.make_async_remote_copy(
+            src_ref=mixed.at[a, pl.ds(h * HALF, HALF)], dst_ref=landed.at[way, e],
+            send_sem=ici_send.at[way, i], recv_sem=ici_recv.at[way, i],
+            device_id={"fsdp_0": target}, device_id_type=MESH,
+        )
+
+    def across(send, recv, shard, a, h):
+        ref = chunk(shard, a, h)
+        return pltpu.make_async_remote_copy(
+            src_ref=ref, dst_ref=ref, send_sem=send, recv_sem=recv,
+            device_id={"fsdp_1": 1 - c}, device_id_type=MESH,
+        )
 
     loads = [pltpu.make_async_copy(share, share_v, in_sem.at[6])]
     loads += [
@@ -96,7 +135,7 @@
     piece = pltpu.roll(jnp.broadcast_to(piece, (8, LANES)), lax.rem(col, 8) * PIECE, 1)
     msg[pl.ds(6, 1), :] = piece[:1]
 
-    pl.semaphore_wait(barrier, SHARDS - 1 + PLANE - 1)
+    pl.semaphore_wait(barrier, SHARDS - 1 + (col + PLANE - 1) // PLANE)
 
     exchanges = []
     for device, p in fsdp_peers():
@@ -106,6 +145,12 @@
         )
         copy.start()
         exchanges.append(copy)
+    sent = list(exchanges)
+    for e in range(len(EARLY)):
+        for way in range(2):
+            copy = early(way, e)
+            copy.start()
+            sent.append(copy)
     sums[pl.ds(me, 1)] = msg[...][None]
     arrivals = []
     for device, p in fsdp_peers():
@@ -121,40 +166,21 @@
         total = total + sums[s]
     scale = jnp.sqrt(total)
     inverse = 1.0 / scale
-    own = pl.multiple_of(me * ROWS, ROWS)
-    for a, out in enumerate(outs):
-        for r in range(2):
-            for j in range(2):
-                lanes = pl.ds(j * LANES, LANES)
-                value = mixed[a, pl.ds(r * HALF, HALF), lanes] * inverse[2 * a + j : 2 * a + j + 1]
-                out[pl.ds(pl.multiple_of(own + r * HALF, HALF), HALF), lanes] = value.astype(jnp.bfloat16)
-
-    def chunk(shard, a, h):
-        return outs[a].at[pl.ds(pl.multiple_of(shard * ROWS + h * HALF, HALF), HALF)]
-
-    def along(way, i):
-        d, a, h = STREAM[way][i]
-        source = lax.rem(z + (Z - d if way == 0 else d), Z)
-        return source * CORES + c, a, h
-
-    def hop(way, i, shard, a, h):
-        ref = chunk(shard, a, h)
-        target = lax.rem(z + (1 if way == 0 else Z - 1), Z)
-        return pltpu.make_async_remote_copy(
-            src_ref=ref, dst_ref=ref, send_sem=ici_send.at[way, i], recv_sem=ici_recv.at[way, i],
-            device_id={"fsdp_0": target}, device_id_type=MESH,
-        )
-
-    def across(send, recv, shard, a, h):
-        ref = chunk(shard, a, h)
-        return pltpu.make_async_remote_copy(
-            src_ref=ref, dst_ref=ref, send_sem=send, recv_sem=recv,
-            device_id={"fsdp_1": 1 - c}, device_id_type=MESH,
-        )
-
-    sent = list(exchanges)
+
+    def put(shard, a, h, read):
+        rows = pl.ds(pl.multiple_of(shard * ROWS + h * HALF, HALF), HALF)
+        for j in range(2):
+            lanes = pl.ds(j * LANES, LANES)
+            value = read(lanes) * inverse[2 * a + j : 2 * a + j + 1]
+            outs[a][rows, lanes] = value.astype(jnp.bfloat16)
+
+    for a, h in sorted(((a, h) for a in range(3) for h in range(2)), key=lambda piece: piece in EARLY):
+        put(me, a, h, lambda lanes: mixed[a, pl.ds(h * HALF, HALF), lanes])
+
     for a in range(3):
         for h in range(2):
+            if (a, h) in EARLY:
+                continue
             for way in range(2):
                 copy = hop(way, 2 * a + h, me, a, h)
                 copy.start()
@@ -171,20 +197,46 @@
 
     for s in range(SHARDS):
         plane_out[pl.ds(s, 1), :] = sums[s, 6:7, :]
-    for device, p in plane_peers():
-        copy = pltpu.make_async_remote_copy(
-            src_ref=plane_out, dst_ref=plane_in.at[col], send_sem=plane_send.at[p], recv_sem=plane_recv.at[col],
+    def to_root(p):
+        return pltpu.make_async_remote_copy(
+            src_ref=plane_out, dst_ref=plane_in.at[p], send_sem=plane_send, recv_sem=plane_recv.at[p],
+            device_id={"cols_0": 0, "cols_1": 0}, device_id_type=MESH,
+        )
+
+    def answer(device, p):
+        return pltpu.make_async_remote_copy(
+            src_ref=norm_f32, dst_ref=norm_f32, send_sem=answer_send.at[p], recv_sem=answer_recv,
             device_id=device, device_id_type=MESH,
         )
-        copy.start()
-        sent.append(copy)
-    plane_in[pl.ds(col, 1)] = plane_out[...][None]
+
+    @pl.when(col > 0)
+    def _():
+        to_root(col).start()
+
+    def answer_all():
+        plane_in[0] = plane_out[...]
+        for _, p in plane_peers():
+            to_root(p).wait_recv()
+        for side in range(2):
+            gathered = plane_in[8 * side]
+            for k in range(1, 8):
+                gathered = gathered + plane_in[8 * side + k]
+            norm_f32[pl.ds(side, SHARDS, stride=2), :] = gathered
+        for device, p in plane_peers():
+            answer(device, p).start()
 
     for i in range(STEPS):
+        if i == ANSWER:
+            pl.when(col == 0)(answer_all)
         for way in range(2):
             d, a, h = STREAM[way][i]
             shard, _, _ = along(way, i)
-            hop(way, i, shard, a, h).wait_recv()
+            if d == 1 and (a, h) in EARLY:
+                e = EARLY.index((a, h))
+                early(way, e).wait_recv()
+                put(shard, a, h, lambda lanes: landed[way, e, :, lanes])
+            else:
+                hop(way, i, shard, a, h).wait_recv()
             if (d + 1, a, h) in STREAM[way]:
                 copy = hop(way, STREAM[way].index((d + 1, a, h)), shard, a, h)
                 copy.start()
@@ -193,17 +245,17 @@
             copy.start()
             sent.append(copy)
 
-    for device, p in plane_peers():
-        pltpu.make_async_remote_copy(
-            src_ref=plane_out, dst_ref=plane_in.at[p], send_sem=plane_send.at[p], recv_sem=plane_recv.at[p],
-            device_id=device, device_id_type=MESH,
-        ).wait_recv()
-    for side in range(2):
-        gathered = plane_in[8 * side]
-        for k in range(1, 8):
-            gathered = gathered + plane_in[8 * side + k]
-        norm_f32[pl.ds(side, SHARDS, stride=2), :] = gathered
+    @pl.when(col > 0)
+    def _():
+        answer({"cols_0": 0, "cols_1": 0}, 0).wait_recv()
+        to_root(col).wait_send()
+
     norm[...] = norm_f32[...].astype(jnp.bfloat16)
+
+    @pl.when(col == 0)
+    def _():
+        for device, p in plane_peers():
+            answer(device, p).wait_send()
 
     partner = z * CORES + 1 - c
     for a in range(3):
@@ -264,6 +316,7 @@
             pltpu.VMEM((1, ROWS), f32),
             pltpu.VMEM((2, 1, PIECE), f32),
             pltpu.VMEM((3, ROWS, 2 * LANES), f32),
+            pltpu.VMEM((2, len(EARLY), HALF, 2 * LANES), f32),
             pltpu.VMEM((8, LANES), f32),
             pltpu.VMEM((SHARDS, 8, LANES), f32),
             pltpu.VMEM((SHARDS, LANES), f32),
@@ -272,8 +325,10 @@
             dma((9,)),
             dma((SHARDS,)),
             dma((SHARDS,)),
+            dma,
             dma((PLANE,)),
             dma((PLANE,)),
+            dma,
             dma((2, STEPS)),
             dma((2, STEPS)),
             dma((6,)),

time: 54.7 us -> 51.3 us (0.938)
  Pallas kernels: 54 us -> 50.5 us
    pallas_call x1, Pallas kernels: 51.2 us -> 47.7 us  [per_device(): pl.pallas_call(kernel, name='mix_and_gather', out_shape=(whole, whole, wh...]
where the time goes in v3:
time: 51.3 us; the launch traced here: 51.2 us
  Pallas kernels  50.5 us (98%)
  between operations  0.64 us (1%)
    pallas_call x1, Pallas kernels, per_device(): pl.pallas_call(kernel, name='mix_and_gather', out_shape=(whole, whole, wh...  47.7 us
    pallas_call x1, Pallas kernels, store(): pl.pallas_call(store_kernel, name='store', out_shape=tuple((jax.ShapeDtyp...  2.8 us

profile of v3, /device:TPU:1, one launch (start us, length us, event | category | flops | bytes accessed | tf_op | source)
XLA Modules:
  0.0 51.2 jit_solution(11785585127996057435)
XLA Ops:
  0.6 47.7 %mix_and_gather.1 = (bf16[4096,256]{1,0:T(8,128)(2,1)S(1)}, bf16[4096,256]{1,0:T(8,128)(2,1)S(1)}, bf16[4096,256]{1,0:T(8,128)(2,1)S(1)}, f32[1,256]{1,0:T(1,128...) custom-call(f32[256,256]{1,0:T(8,128)} %oq.1, f32[256,256]{1,0:T(8,128)} %tq.1, ...), custom_call_target="tpu_custom_call" | custom-call | tf_op jit(solution)/shard_map/mix_and_gather/pallas_call | solution.py:308
  48.4 2.8 %store.1 = (bf16[4096,256]{1,0:T(8,128)(2,1)}, bf16[4096,256]{1,0:T(8,128)(2,1)}, bf16[4096,256]{1,0:T(8,128)(2,1)}, f32[1,256]{1,0:T(1,128)}, f32[1,256]{1,0:T(...) custom-call(bf16[4096,256]{1,0:T(8,128)(2,1)S(1)} %get-tuple-element.21.refs_0_, ...), custom_call_target="tpu_custom_call" | custom-call | tf_op jit(solution)/shard_map/store/pallas_call | solution.py:291

commit v4 on v3

v4 whole, which is shorter than its diff:
```python
import functools

import jax
import jax.numpy as jnp
from jax import lax
from jax.experimental import pallas as pl
from jax.experimental.pallas import tpu as pltpu
from jax.sharding import Mesh
from jax.sharding import PartitionSpec as P

FSDP = ("fsdp_0", "fsdp_1")
FSDP_COLS = ("fsdp_0", "fsdp_1", "cols_0", "cols_1")
COLS = ("cols_0", "cols_1")
MESH = pl.DeviceIdType.MESH

Z = 8
CORES = 2
SHARDS = Z * CORES
PLANE_Y = 4
PLANE_X = 4
PLANE = PLANE_Y * PLANE_X
ROWS = 256
HALF = 128
LANES = 128
PIECE = 16

EARLY = [(0, 0, 128), (0, 128, 64)]
EARLY_ROWS = sum(n for _, _, n in EARLY)
LATE = [(0, EARLY_ROWS, ROWS - EARLY_ROWS), (1, 0, ROWS), (2, 0, ROWS)]
WHOLE = [(a, 0, ROWS) for a in range(3)]
CROSS = (0, HALF)
BASE = tuple(
    [(1, p) for p in EARLY + LATE]
    + [(2, p) for p in WHOLE]
    + [(3, p) for p in WHOLE[:2] + [(2, CROSS[way], HALF), (2, CROSS[1 - way], HALF)]]
    for way in (0, 1)
)
STEPS = len(BASE[0])
LAST = [(a, other) for a in range(3) for other in (0, 1)]
TAIL = len(LAST)
ANSWER = 5
LAG = 1
PARTS = 4


def kernel(
    oq, tq, ok, tk, ov, tv, share, train, step,
    out_q, out_k, out_v, scale_q, scale_k, scale_v, norm,
    ins, share_v, norm_in, mixed, landed, msg, sums, plane_out, plane_in, norm_f32,
    in_sem, sum_send, sum_recv, plane_send, plane_recv, answer_send, answer_recv,
    early_send, ici_send, ici_recv, push_send, push_recv, cross_recv,
):
    z, c = lax.axis_index("fsdp_0"), lax.axis_index("fsdp_1")
    col = lax.axis_index("cols_0") * PLANE_X + lax.axis_index("cols_1")
    me = z * CORES + c
    outs = (out_q, out_k, out_v)

    def fsdp_peers():
        for dz in (4, 5, 3, 6, 2, 7, 1, 0):
            for dc in (0, 1):
                if dz or dc:
                    pz, pc = lax.rem(z + dz, Z), lax.rem(c + dc, CORES)
                    yield {"fsdp_0": pz, "fsdp_1": pc}, pz * CORES + pc

    def plane_peers():
        for p in range(1, PLANE):
            yield {"cols_0": p // PLANE_X, "cols_1": p % PLANE_X}, p

    barrier = pltpu.get_barrier_semaphore()
    for device, _ in fsdp_peers():
        pl.semaphore_signal(barrier, inc=1, device_id=device, device_id_type=MESH)

    pltpu.make_async_copy(share, share_v, in_sem.at[3]).start()
    for i, src in enumerate((oq, tq, ok, tk, ov, tv)):
        pltpu.make_async_copy(src, ins.at[i], in_sem.at[i // 2]).start()
    for i, src in enumerate((train, step)):
        pltpu.make_async_copy(src, norm_in.at[i], in_sem.at[4]).start()

    @pl.when(col == 0)
    def _():
        for device, _ in plane_peers():
            pl.semaphore_signal(barrier, inc=1, device_id=device, device_id_type=MESH)

    def place(shard, piece):
        a, r, n = piece
        return outs[a].at[pl.ds(pl.multiple_of(shard * ROWS + r, n), n)]

    def shard_of(way, d, core):
        return lax.rem(z + (Z - d if way == 0 else d), Z) * CORES + core

    def hop(way, i, src, dst, send):
        target = lax.rem(z + (1 if way == 0 else Z - 1), Z)
        return pltpu.make_async_remote_copy(
            src_ref=src, dst_ref=dst, send_sem=send, recv_sem=ici_recv.at[way, i],
            device_id={"fsdp_0": target}, device_id_type=MESH,
        )

    def early(way, i):
        a, r, n = EARLY[i]
        return hop(way, i, mixed.at[a, pl.ds(r, n)], landed.at[way, pl.ds(r, n)], early_send)

    def ring(way, i, shard):
        piece = BASE[way][i][1]
        ref = place(shard, piece)
        return hop(way, i, ref, ref, ici_send.at[piece[0]])

    def last(way, t, d):
        a, other = LAST[t]
        core = lax.rem(c + other, CORES)
        ref = place(shard_of(way, d, core), (a, CROSS[way], HALF))
        return hop(way, STEPS + t, ref, ref, ici_send.at[a])

    def across(ref, a, recv):
        return pltpu.make_async_remote_copy(
            src_ref=ref, dst_ref=ref, send_sem=push_send.at[a], recv_sem=recv,
            device_id={"fsdp_1": 1 - c}, device_id_type=MESH,
        )

    def push(shard, piece):
        return across(place(shard, piece), piece[0], push_recv.at[piece[0]])

    def rows_of(a, rows):
        return outs[a].at[pl.ds(0, rows)]

    msg[...] = jnp.zeros_like(msg)
    pltpu.make_async_copy(share, share_v, in_sem.at[3]).wait()
    shares = [
        jnp.broadcast_to(share_v[:, r * HALF : (r + 1) * HALF], (LANES, HALF)).T for r in range(2)
    ]
    for a in range(3):
        pair = ins.at[pl.ds(2 * a, 2)]
        pltpu.make_async_copy(pair, pair, in_sem.at[a]).wait()
        for j in range(2):
            lanes = pl.ds(j * LANES, LANES)
            total = jnp.zeros((1, LANES), jnp.float32)
            for r in range(2):
                rows = pl.ds(r * HALF, HALF)
                value = shares[r] * ins[2 * a, rows, lanes] + (1.0 - shares[r]) * ins[2 * a + 1, rows, lanes]
                mixed[a, rows, lanes] = value
                total = total + jnp.sum(value * value, axis=0, keepdims=True)
            msg[pl.ds(2 * a + j, 1), :] = total
    pltpu.make_async_copy(norm_in, norm_in, in_sem.at[4]).wait()
    piece = jnp.concatenate(
        [norm_in[0] + norm_in[1], jnp.zeros((1, LANES - PIECE), jnp.float32)], axis=1
    )
    piece = pltpu.roll(jnp.broadcast_to(piece, (8, LANES)), lax.rem(col, 8) * PIECE, 1)
    msg[pl.ds(6, 1), :] = piece[:1]

    pl.semaphore_wait(barrier, SHARDS - 1 + (col + PLANE - 1) // PLANE)

    def message(device, slot):
        return pltpu.make_async_remote_copy(
            src_ref=msg, dst_ref=sums.at[slot], send_sem=sum_send, recv_sem=sum_recv,
            device_id=device, device_id_type=MESH,
        )

    for device, _ in fsdp_peers():
        message(device, me).start()
    for i in range(len(EARLY)):
        for way in range(2):
            early(way, i).start()
    sums[pl.ds(me, 1)] = msg[...][None]

    def all_messages(slots):
        return pltpu.make_async_remote_copy(
            src_ref=slots, dst_ref=slots, send_sem=sum_send, recv_sem=sum_recv,
            device_id={"fsdp_1": 1 - c}, device_id_type=MESH,
        )

    all_messages(sums.at[pl.ds(0, SHARDS - 1)]).wait_recv()

    total = sums[0]
    for s in range(1, SHARDS):
        total = total + sums[s]
    scale = jnp.sqrt(total)
    inverse = 1.0 / scale

    def put(shard, piece, read):
        a, r, n = piece
        rows = pl.ds(pl.multiple_of(shard * ROWS + r, n), n)
        for j in range(2):
            lanes = pl.ds(j * LANES, LANES)
            value = read(lanes) * inverse[2 * a + j : 2 * a + j + 1]
            outs[a][rows, lanes] = value.astype(jnp.bfloat16)

    for piece in LATE + EARLY:
        a, r, n = piece
        put(me, piece, lambda lanes: mixed[a, pl.ds(r, n), lanes])
    for i in range(len(EARLY), len(EARLY + LATE)):
        for way in range(2):
            ring(way, i, me).start()
    for piece in WHOLE:
        push(me, piece).start()

    for a, ref in enumerate((scale_q, scale_k, scale_v)):
        for j in range(2):
            ref[:, pl.ds(j * LANES, LANES)] = scale[2 * a + j : 2 * a + j + 1]

    for s in range(SHARDS):
        plane_out[pl.ds(s, 1), :] = sums[s, 6:7, :]

    def to_root(p):
        return pltpu.make_async_remote_copy(
            src_ref=plane_out, dst_ref=plane_in.at[p], send_sem=plane_send, recv_sem=plane_recv,
            device_id={"cols_0": 0, "cols_1": 0}, device_id_type=MESH,
        )

    def answer(device):
        return pltpu.make_async_remote_copy(
            src_ref=norm_f32, dst_ref=norm_f32, send_sem=answer_send, recv_sem=answer_recv,
            device_id=device, device_id_type=MESH,
        )

    @pl.when(col > 0)
    def _():
        to_root(col).start()

    def answer_all():
        plane_in[0] = plane_out[...]
        pieces = plane_in.at[pl.ds(1, PLANE - 1)]
        pltpu.make_async_remote_copy(
            src_ref=pieces, dst_ref=pieces, send_sem=plane_send, recv_sem=plane_recv,
            device_id={"cols_0": 0, "cols_1": 1}, device_id_type=MESH,
        ).wait_recv()
        for side in range(2):
            gathered = plane_in[8 * side]
            for k in range(1, 8):
                gathered = gathered + plane_in[8 * side + k]
            norm_f32[pl.ds(side, SHARDS, stride=2), :] = gathered
        for device, _ in plane_peers():
            answer(device).start()

    def onward(way, i):
        d, (a, r, n) = BASE[way][i]
        if d == 1 and r + n == ROWS or d == 2:
            for k, (far, piece) in enumerate(BASE[way]):
                if far == d + 1 and piece[0] == a:
                    ring(way, k, shard_of(way, d, c)).start()

    def crosses(way, i):
        d, (a, r, n) = BASE[way][i]
        return d == 3 and r <= CROSS[way] < r + n

    def from_partner(way, i):
        _, piece = BASE[way][i]
        a = piece[0]
        across(place(shard_of(way, 3, 1 - c), piece), a, cross_recv.at[way, a]).wait_recv()
        last(way, LAST.index((a, 1)), 3).start()

    for i in range(STEPS + LAG):
        if i == ANSWER:
            pl.when(col == 0)(answer_all)
        if i < STEPS:
            for way in range(2):
                d, piece = BASE[way][i]
                a = piece[0]
                shard = shard_of(way, d, c)
                if d == 1 and piece in EARLY:
                    early(way, i).wait_recv()
                    put(shard, piece, lambda lanes: landed[way, pl.ds(piece[1], piece[2]), lanes])
                else:
                    ring(way, i, shard).wait_recv()
                onward(way, i)
                if crosses(way, i):
                    @pl.when(c == 1)
                    def _():
                        last(way, LAST.index((a, 0)), 3).start()
                        push(shard, piece).start()

                    @pl.when(c == 0)
                    def _():
                        across(place(shard, piece), a, cross_recv.at[way, a]).start()
                else:
                    push(shard, piece).start()
        for way in range(2):
            if i >= LAG and crosses(way, i - LAG):
                pl.when(c == 1)(functools.partial(from_partner, way, i - LAG))

    @pl.when(c == 1)
    def _():
        for t, (a, other) in enumerate(LAST):
            for way in range(2):
                last(way, t, 4).wait_recv()
                push(shard_of(way, 4, lax.rem(c + other, CORES)), (a, CROSS[way], HALF)).start()

    @pl.when(col > 0)
    def _():
        answer({"cols_0": 0, "cols_1": 0}).wait_recv()
        to_root(col).wait_send()

    norm[...] = norm_f32[...].astype(jnp.bfloat16)

    @pl.when(col == 0)
    def _():
        ref = ins.at[0, pl.ds(0, 16 * (PLANE - 1))]
        pltpu.make_async_remote_copy(
            src_ref=ref, dst_ref=ref, send_sem=answer_send, recv_sem=answer_recv,
            device_id={"cols_0": 0, "cols_1": 1}, device_id_type=MESH,
        ).wait_send()

    all_messages(sums.at[pl.ds(0, SHARDS - 1)]).wait_send()
    ref = ins.at[pl.ds(0, 2), pl.ds(0, EARLY_ROWS)]
    hop(0, 0, ref, ref, early_send).wait_send()

    def finish(core):
        def _():
            for a in range(3):
                own = ROWS - (EARLY_ROWS if a == 0 else 0)
                ring_rows = 2 * (own + 2 * ROWS + (ROWS if core else 0))
                pushed = ROWS + 2 * (3 * ROWS + (ROWS if core else 0))
                crossing = sum(p[2] for way in (0, 1) for i, (_, p) in enumerate(BASE[way]) if crosses(way, i) and p[0] == a)
                come = ROWS + 2 * 3 * ROWS + (-crossing if core else 2 * ROWS)
                ref = rows_of(a, come)
                across(ref, a, push_recv.at[a]).wait_recv()
                ref = rows_of(a, ring_rows)
                hop(0, 0, ref, ref, ici_send.at[a]).wait_send()
                ref = rows_of(a, pushed)
                across(ref, a, push_recv.at[a]).wait_send()

        return _

    for core in range(CORES):
        pl.when(c == core)(finish(core))


def store_kernel(*refs):
    ins, outs, sem = refs[:7], refs[7:14], refs[14]
    for i, (src, dst) in enumerate(zip(ins, outs)):
        parts = PARTS if i < 3 else 1
        rows = src.shape[0] // parts
        for p in range(parts):
            window = pl.ds(p * rows, rows)
            pltpu.make_async_copy(src.at[window], dst.at[window], sem.at[i]).start()
    for i, (src, dst) in enumerate(zip(ins, outs)):
        pltpu.make_async_copy(src, dst, sem.at[i]).wait()


def store(arrays):
    return pl.pallas_call(
        store_kernel,
        name="store",
        out_shape=tuple(jax.ShapeDtypeStruct(a.shape, a.dtype) for a in arrays),
        in_specs=[pl.BlockSpec(memory_space=pltpu.VMEM)] * 7,
        out_specs=(pl.BlockSpec(memory_space=pltpu.HBM),) * 7,
        scratch_shapes=[pltpu.SemaphoreType.DMA((7,))],
        compiler_params=pltpu.CompilerParams(vmem_limit_bytes=16 * 2**20),
    )(*arrays)


def per_device(oq, tq, ok, tk, ov, tv, share, train, step):
    f32, bf16 = jnp.float32, jnp.bfloat16
    whole = jax.ShapeDtypeStruct((SHARDS * ROWS, 2 * LANES), bf16)
    scale = jax.ShapeDtypeStruct((1, 2 * LANES), f32)
    vmem = pl.BlockSpec(memory_space=pltpu.VMEM)
    dma = pltpu.SemaphoreType.DMA
    outs = pl.pallas_call(
        kernel,
        name="mix_and_gather",
        out_shape=(whole, whole, whole, scale, scale, scale, jax.ShapeDtypeStruct((32, LANES), bf16)),
        in_specs=[pl.BlockSpec(memory_space=pltpu.HBM)] * 9,
        out_specs=(vmem,) * 7,
        scratch_shapes=[
            pltpu.VMEM((6, ROWS, 2 * LANES), f32),
            pltpu.VMEM((1, ROWS), f32),
            pltpu.VMEM((2, 1, PIECE), f32),
            pltpu.VMEM((3, ROWS, 2 * LANES), f32),
            pltpu.VMEM((2, EARLY_ROWS, 2 * LANES), f32),
            pltpu.VMEM((8, LANES), f32),
            pltpu.VMEM((SHARDS, 8, LANES), f32),
            pltpu.VMEM((SHARDS, LANES), f32),
            pltpu.VMEM((PLANE, SHARDS, LANES), f32),
            pltpu.VMEM((32, LANES), f32),
            dma((5,)),
            dma,
            dma,
            dma,
            dma,
            dma,
            dma,
            dma,
            dma((3,)),
            dma((2, STEPS + TAIL)),
            dma((3,)),
            dma((3,)),
            dma((2, 3)),
        ],
        compiler_params=pltpu.CompilerParams(
            collective_id=0, has_side_effects=True, vmem_limit_bytes=24 * 2**20
        ),
    )(*(pltpu.with_memory_space_constraint(a, pltpu.HBM) for a in (
        oq, tq, ok, tk, ov, tv, share.reshape(1, -1), train.reshape(1, -1), step.reshape(1, -1)
    )))
    q, k, v, scale_q, scale_k, scale_v, norm = store(outs)
    return q, k, v, scale_q.reshape(-1), scale_k.reshape(-1), scale_v.reshape(-1), norm.reshape(-1)


def solution(mesh):
    split = Mesh(mesh.devices.reshape(Z, CORES, PLANE_Y, PLANE_X), FSDP_COLS)
    block = P(FSDP, COLS)
    return jax.shard_map(
        per_device,
        mesh=split,
        in_specs=(block,) * 6 + (P(FSDP), P(FSDP_COLS), P(FSDP_COLS)),
        out_specs=(P(None, COLS),) * 3 + (P(COLS),) * 3 + (P(),),
        check_vma=False,
    )
```

time: 51.3 us -> 48.1 us (0.938)
  Pallas kernels: 50.5 us -> 47.3 us
    pallas_call x1, Pallas kernels: 47.7 us -> 44.6 us  [per_device(): pl.pallas_call(kernel, name='mix_and_gather', out_shape=(whole, whole, wh...]
where the time goes in v4:
time: 48.1 us; the launch traced here: 48 us
  Pallas kernels  47.3 us (98%)
  between operations  0.64 us (1%)
    pallas_call x1, Pallas kernels, per_device(): pl.pallas_call(kernel, name='mix_and_gather', out_shape=(whole, whole, wh...  44.6 us
    pallas_call x1, Pallas kernels, store(): pl.pallas_call(store_kernel, name='store', out_shape=tuple((jax.ShapeDtyp...  2.72 us

profile of v4, /device:TPU:1, one launch (start us, length us, event | category | flops | bytes accessed | tf_op | source)
XLA Modules:
  0.0 48.0 jit_solution(9898247265472672279)
XLA Ops:
  0.6 44.6 %mix_and_gather.1 = (bf16[4096,256]{1,0:T(8,128)(2,1)S(1)}, bf16[4096,256]{1,0:T(8,128)(2,1)S(1)}, bf16[4096,256]{1,0:T(8,128)(2,1)S(1)}, f32[1,256]{1,0:T(1,128...) custom-call(f32[256,256]{1,0:T(8,128)} %oq.1, f32[256,256]{1,0:T(8,128)} %tq.1, ...), custom_call_target="tpu_custom_call" | custom-call | tf_op jit(solution)/shard_map/mix_and_gather/pallas_call | solution.py:356
  45.3 2.7 %store.1 = (bf16[4096,256]{1,0:T(8,128)(2,1)}, bf16[4096,256]{1,0:T(8,128)(2,1)}, bf16[4096,256]{1,0:T(8,128)(2,1)}, f32[1,256]{1,0:T(1,128)}, f32[1,256]{1,0:T(...) custom-call(bf16[4096,256]{1,0:T(8,128)(2,1)S(1)} %get-tuple-element.21.refs_0_, ...), custom_call_target="tpu_custom_call" | custom-call | tf_op jit(solution)/shard_map/store/pallas_call | solution.py:339

commit v5 on v4

--- a/solution.py
+++ b/solution.py
@@ -1,4 +1,5 @@
 import functools
+import math
 
 import jax
 import jax.numpy as jnp
@@ -24,21 +25,28 @@
 LANES = 128
 PIECE = 16
 
-EARLY = [(0, 0, 128), (0, 128, 64)]
-EARLY_ROWS = sum(n for _, _, n in EARLY)
-LATE = [(0, EARLY_ROWS, ROWS - EARLY_ROWS), (1, 0, ROWS), (2, 0, ROWS)]
 WHOLE = [(a, 0, ROWS) for a in range(3)]
-CROSS = (0, HALF)
+FIRST = (
+    [(0, 0, ROWS), (1, 0, ROWS), (2, 0, ROWS)],
+    [(0, 0, HALF), (0, HALF, HALF), (1, 0, ROWS), (2, 0, ROWS)],
+)
+EARLY = (1, 1)
+SPLIT = 128
+CROSS = ((0, SPLIT), (SPLIT, ROWS - SPLIT))
 BASE = tuple(
-    [(1, p) for p in EARLY + LATE]
+    [(1, p) for p in range(max(len(f) for f in FIRST))]
     + [(2, p) for p in WHOLE]
-    + [(3, p) for p in WHOLE[:2] + [(2, CROSS[way], HALF), (2, CROSS[1 - way], HALF)]]
+    + [(3, p) for p in WHOLE[:2] + [(2, *CROSS[way]), (2, *CROSS[1 - way])]]
     for way in (0, 1)
 )
+NEAR = sum(d == 1 for d, _ in BASE[0])
+EARLY_AT = [[sum(n for _, _, n in f[:i]) for i in range(e + 1)] for f, e in zip(FIRST, EARLY)]
+EARLY_ROWS = max(at[-1] for at in EARLY_AT)
 STEPS = len(BASE[0])
 LAST = [(a, other) for a in range(3) for other in (0, 1)]
 TAIL = len(LAST)
-ANSWER = 5
+ANSWER = 4
+PASS = 7
 LAG = 1
 PARTS = 4
 
@@ -46,8 +54,8 @@
 def kernel(
     oq, tq, ok, tk, ov, tv, share, train, step,
     out_q, out_k, out_v, scale_q, scale_k, scale_v, norm,
-    ins, share_v, norm_in, mixed, landed, msg, sums, plane_out, plane_in, norm_f32,
-    in_sem, sum_send, sum_recv, plane_send, plane_recv, answer_send, answer_recv,
+    ins, share_v, norm_in, mixed, landed, msg, both, total_v, sums, plane_out, plane_in, norm_f32,
+    in_sem, chip_send, chip_recv, sum_send, sum_recv, plane_send, plane_recv, answer_send, answer_recv,
     early_send, ici_send, ici_recv, push_send, push_recv, cross_recv,
 ):
     z, c = lax.axis_index("fsdp_0"), lax.axis_index("fsdp_1")
@@ -55,20 +63,33 @@
     me = z * CORES + c
     outs = (out_q, out_k, out_v)
 
-    def fsdp_peers():
-        for dz in (4, 5, 3, 6, 2, 7, 1, 0):
-            for dc in (0, 1):
-                if dz or dc:
-                    pz, pc = lax.rem(z + dz, Z), lax.rem(c + dc, CORES)
-                    yield {"fsdp_0": pz, "fsdp_1": pc}, pz * CORES + pc
+    ahead, behind = lax.rem(z + 1, Z), lax.rem(z + Z - 1, Z)
+    partner = {"fsdp_1": 1 - c}
+
+    def far_peers():
+        for dz in (4, 5, 3, 6, 2, 7, 1):
+            yield {"fsdp_0": lax.rem(z + dz, Z)}
 
     def plane_peers():
         for p in range(1, PLANE):
-            yield {"cols_0": p // PLANE_X, "cols_1": p % PLANE_X}, p
+            yield {"cols_0": p // PLANE_X, "cols_1": p % PLANE_X}
 
     barrier = pltpu.get_barrier_semaphore()
-    for device, _ in fsdp_peers():
+
+    def greet(device):
         pl.semaphore_signal(barrier, inc=1, device_id=device, device_id_type=MESH)
+
+    @pl.when(c == 0)
+    def _():
+        for target in (ahead, behind):
+            greet({"fsdp_0": target})
+
+    @pl.when(c == 1)
+    def _():
+        for device in far_peers():
+            greet(device)
+
+    greet(partner)
 
     pltpu.make_async_copy(share, share_v, in_sem.at[3]).start()
     for i, src in enumerate((oq, tq, ok, tk, ov, tv)):
@@ -76,44 +97,49 @@
     for i, src in enumerate((train, step)):
         pltpu.make_async_copy(src, norm_in.at[i], in_sem.at[4]).start()
 
-    @pl.when(col == 0)
-    def _():
-        for device, _ in plane_peers():
-            pl.semaphore_signal(barrier, inc=1, device_id=device, device_id_type=MESH)
+    @pl.when(c * PLANE + col == PLANE)
+    def _():
+        for device in plane_peers():
+            greet(device)
 
     def place(shard, piece):
         a, r, n = piece
-        return outs[a].at[pl.ds(pl.multiple_of(shard * ROWS + r, n), n)]
+        return outs[a].at[pl.ds(pl.multiple_of(shard * ROWS + r, math.gcd(ROWS, r, n)), n)]
 
     def shard_of(way, d, core):
         return lax.rem(z + (Z - d if way == 0 else d), Z) * CORES + core
 
     def hop(way, i, src, dst, send):
-        target = lax.rem(z + (1 if way == 0 else Z - 1), Z)
+        target = ahead if way == 0 else behind
         return pltpu.make_async_remote_copy(
             src_ref=src, dst_ref=dst, send_sem=send, recv_sem=ici_recv.at[way, i],
             device_id={"fsdp_0": target}, device_id_type=MESH,
         )
 
-    def early(way, i):
-        a, r, n = EARLY[i]
-        return hop(way, i, mixed.at[a, pl.ds(r, n)], landed.at[way, pl.ds(r, n)], early_send)
+    def early(way, i, core):
+        a, r, n = FIRST[core][i]
+        return hop(way, i, mixed.at[a, pl.ds(r, n)], landed.at[way, pl.ds(EARLY_AT[core][i], n)], early_send)
 
     def ring(way, i, shard):
         piece = BASE[way][i][1]
         ref = place(shard, piece)
         return hop(way, i, ref, ref, ici_send.at[piece[0]])
 
+    def first(way, i, core, shard):
+        piece = FIRST[core][i]
+        ref = place(shard, piece)
+        return hop(way, i, ref, ref, ici_send.at[piece[0]])
+
     def last(way, t, d):
         a, other = LAST[t]
         core = lax.rem(c + other, CORES)
-        ref = place(shard_of(way, d, core), (a, CROSS[way], HALF))
+        ref = place(shard_of(way, d, core), (a, *CROSS[way]))
         return hop(way, STEPS + t, ref, ref, ici_send.at[a])
 
     def across(ref, a, recv):
         return pltpu.make_async_remote_copy(
             src_ref=ref, dst_ref=ref, send_sem=push_send.at[a], recv_sem=recv,
-            device_id={"fsdp_1": 1 - c}, device_id_type=MESH,
+            device_id=partner, device_id_type=MESH,
         )
 
     def push(shard, piece):
@@ -144,51 +170,73 @@
         [norm_in[0] + norm_in[1], jnp.zeros((1, LANES - PIECE), jnp.float32)], axis=1
     )
     piece = pltpu.roll(jnp.broadcast_to(piece, (8, LANES)), lax.rem(col, 8) * PIECE, 1)
-    msg[pl.ds(6, 1), :] = piece[:1]
-
-    pl.semaphore_wait(barrier, SHARDS - 1 + (col + PLANE - 1) // PLANE)
-
-    def message(device, slot):
-        return pltpu.make_async_remote_copy(
-            src_ref=msg, dst_ref=sums.at[slot], send_sem=sum_send, recv_sem=sum_recv,
+    msg[pl.ds(6 + c, 1), :] = piece[:1]
+
+    def over_chip(src, dst):
+        return pltpu.make_async_remote_copy(
+            src_ref=src, dst_ref=dst, send_sem=chip_send, recv_sem=chip_recv,
+            device_id=partner, device_id_type=MESH,
+        )
+
+    def message(device, src, slot):
+        return pltpu.make_async_remote_copy(
+            src_ref=src, dst_ref=slot, send_sem=sum_send, recv_sem=sum_recv,
             device_id=device, device_id_type=MESH,
         )
 
-    for device, _ in fsdp_peers():
-        message(device, me).start()
-    for i in range(len(EARLY)):
-        for way in range(2):
-            early(way, i).start()
-    sums[pl.ds(me, 1)] = msg[...][None]
-
-    def all_messages(slots):
-        return pltpu.make_async_remote_copy(
-            src_ref=slots, dst_ref=slots, send_sem=sum_send, recv_sem=sum_recv,
-            device_id={"fsdp_1": 1 - c}, device_id_type=MESH,
-        )
-
-    all_messages(sums.at[pl.ds(0, SHARDS - 1)]).wait_recv()
-
-    total = sums[0]
-    for s in range(1, SHARDS):
-        total = total + sums[s]
-    scale = jnp.sqrt(total)
+    every = sums.at[pl.ds(0, Z - 1)]
+
+    @pl.when(c == 0)
+    def _():
+        pl.semaphore_wait(barrier, 3)
+        over_chip(msg, both).start()
+        for i in range(EARLY[0]):
+            for way in range(2):
+                early(way, i, 0).start()
+        over_chip(total_v, total_v).wait_recv()
+
+    @pl.when(c == 1)
+    def _():
+        pl.semaphore_wait(barrier, Z + (col + PLANE - 1) // PLANE)
+        over_chip(msg, both).wait_recv()
+        both[...] = both[...] + msg[...]
+        for device in far_peers():
+            message(device, both, sums.at[z]).start()
+        for i in range(EARLY[1]):
+            for way in range(2):
+                early(way, i, 1).start()
+        sums[pl.ds(z, 1)] = both[...][None]
+        message(partner, every, every).wait_recv()
+        total = sums[0]
+        for s in range(1, Z):
+            total = total + sums[s]
+        total_v[...] = total
+        over_chip(total_v, total_v).start()
+
+    scale = jnp.sqrt(total_v[...])
     inverse = 1.0 / scale
 
     def put(shard, piece, read):
         a, r, n = piece
-        rows = pl.ds(pl.multiple_of(shard * ROWS + r, n), n)
+        rows = pl.ds(pl.multiple_of(shard * ROWS + r, math.gcd(ROWS, r, n)), n)
         for j in range(2):
             lanes = pl.ds(j * LANES, LANES)
             value = read(lanes) * inverse[2 * a + j : 2 * a + j + 1]
             outs[a][rows, lanes] = value.astype(jnp.bfloat16)
 
-    for piece in LATE + EARLY:
+    def put_own(piece):
         a, r, n = piece
         put(me, piece, lambda lanes: mixed[a, pl.ds(r, n), lanes])
-    for i in range(len(EARLY), len(EARLY + LATE)):
-        for way in range(2):
-            ring(way, i, me).start()
+
+    for piece in WHOLE:
+        put_own(piece)
+    for core in range(CORES):
+        @pl.when(c == core)
+        def _():
+            for i in range(EARLY[core], len(FIRST[core])):
+                for way in range(2):
+                    first(way, i, core, me).start()
+
     for piece in WHOLE:
         push(me, piece).start()
 
@@ -196,12 +244,9 @@
         for j in range(2):
             ref[:, pl.ds(j * LANES, LANES)] = scale[2 * a + j : 2 * a + j + 1]
 
-    for s in range(SHARDS):
-        plane_out[pl.ds(s, 1), :] = sums[s, 6:7, :]
-
-    def to_root(p):
-        return pltpu.make_async_remote_copy(
-            src_ref=plane_out, dst_ref=plane_in.at[p], send_sem=plane_send, recv_sem=plane_recv,
+    def to_root():
+        return pltpu.make_async_remote_copy(
+            src_ref=plane_out, dst_ref=plane_in.at[col], send_sem=plane_send, recv_sem=plane_recv,
             device_id={"cols_0": 0, "cols_1": 0}, device_id_type=MESH,
         )
 
@@ -211,9 +256,14 @@
             device_id=device, device_id_type=MESH,
         )
 
-    @pl.when(col > 0)
-    def _():
-        to_root(col).start()
+    @pl.when(c == 1)
+    def _():
+        for s in range(SHARDS):
+            plane_out[pl.ds(s, 1), :] = sums[s // CORES, 6 + s % CORES : 7 + s % CORES, :]
+
+    @pl.when((col > 0) & (c == 1))
+    def _():
+        to_root().start()
 
     def answer_all():
         plane_in[0] = plane_out[...]
@@ -227,19 +277,27 @@
             for k in range(1, 8):
                 gathered = gathered + plane_in[8 * side + k]
             norm_f32[pl.ds(side, SHARDS, stride=2), :] = gathered
-        for device, _ in plane_peers():
+        for device in plane_peers():
             answer(device).start()
+        answer(partner).start()
+
+    def pass_on():
+        answer({"cols_0": 0, "cols_1": 0}).wait_recv()
+        answer(partner).start()
 
     def onward(way, i):
-        d, (a, r, n) = BASE[way][i]
-        if d == 1 and r + n == ROWS or d == 2:
-            for k, (far, piece) in enumerate(BASE[way]):
-                if far == d + 1 and piece[0] == a:
-                    ring(way, k, shard_of(way, d, c)).start()
+        d, piece = BASE[way][i]
+        if d == 2:
+            go_on(way, piece[0], 2)
+
+    def go_on(way, a, d):
+        for k, (far, piece) in enumerate(BASE[way]):
+            if far == d + 1 and piece[0] == a:
+                ring(way, k, shard_of(way, d, c)).start()
 
     def crosses(way, i):
-        d, (a, r, n) = BASE[way][i]
-        return d == 3 and r <= CROSS[way] < r + n
+        d, piece = BASE[way][i]
+        return d == 3 and piece[1] <= CROSS[way][0] < piece[1] + piece[2]
 
     def from_partner(way, i):
         _, piece = BASE[way][i]
@@ -247,19 +305,35 @@
         across(place(shard_of(way, 3, 1 - c), piece), a, cross_recv.at[way, a]).wait_recv()
         last(way, LAST.index((a, 1)), 3).start()
 
+    def near(way, i, core):
+        piece = FIRST[core][i]
+        a, r, n = piece
+        shard = shard_of(way, 1, core)
+        if i < EARLY[core]:
+            early(way, i, core).wait_recv()
+            put(shard, piece, lambda lanes: landed[way, pl.ds(EARLY_AT[core][i], n), lanes])
+        else:
+            first(way, i, core, shard).wait_recv()
+        if r + n == ROWS:
+            go_on(way, a, 1)
+        push(shard, piece).start()
+
     for i in range(STEPS + LAG):
         if i == ANSWER:
-            pl.when(col == 0)(answer_all)
+            pl.when(c * PLANE + col == PLANE)(answer_all)
+        if i == PASS:
+            pl.when((col > 0) & (c == 1))(pass_on)
         if i < STEPS:
             for way in range(2):
                 d, piece = BASE[way][i]
+                if d == 1:
+                    for core in range(CORES):
+                        if i < len(FIRST[core]):
+                            pl.when(c == core)(functools.partial(near, way, i, core))
+                    continue
                 a = piece[0]
                 shard = shard_of(way, d, c)
-                if d == 1 and piece in EARLY:
-                    early(way, i).wait_recv()
-                    put(shard, piece, lambda lanes: landed[way, pl.ds(piece[1], piece[2]), lanes])
-                else:
-                    ring(way, i, shard).wait_recv()
+                ring(way, i, shard).wait_recv()
                 onward(way, i)
                 if crosses(way, i):
                     @pl.when(c == 1)
@@ -281,31 +355,40 @@
         for t, (a, other) in enumerate(LAST):
             for way in range(2):
                 last(way, t, 4).wait_recv()
-                push(shard_of(way, 4, lax.rem(c + other, CORES)), (a, CROSS[way], HALF)).start()
-
-    @pl.when(col > 0)
-    def _():
-        answer({"cols_0": 0, "cols_1": 0}).wait_recv()
-        to_root(col).wait_send()
-
-    norm[...] = norm_f32[...].astype(jnp.bfloat16)
-
-    @pl.when(col == 0)
-    def _():
-        ref = ins.at[0, pl.ds(0, 16 * (PLANE - 1))]
+                push(shard_of(way, 4, lax.rem(c + other, CORES)), (a, *CROSS[way])).start()
+
+    @pl.when(c == 1)
+    def _():
+        message(partner, every, every).wait_send()
+        over_chip(total_v, total_v).wait_send()
+
+    @pl.when((col > 0) & (c == 1))
+    def _():
+        to_root().wait_send()
+        answer(partner).wait_send()
+
+    @pl.when(c * PLANE + col == PLANE)
+    def _():
+        ref = ins.at[0, pl.ds(0, 16 * PLANE)]
         pltpu.make_async_remote_copy(
             src_ref=ref, dst_ref=ref, send_sem=answer_send, recv_sem=answer_recv,
-            device_id={"cols_0": 0, "cols_1": 1}, device_id_type=MESH,
+            device_id=partner, device_id_type=MESH,
         ).wait_send()
 
-    all_messages(sums.at[pl.ds(0, SHARDS - 1)]).wait_send()
-    ref = ins.at[pl.ds(0, 2), pl.ds(0, EARLY_ROWS)]
-    hop(0, 0, ref, ref, early_send).wait_send()
+    @pl.when(c == 0)
+    def _():
+        over_chip(msg, both).wait_send()
+        answer(partner).wait_recv()
+
+    norm[...] = norm_f32[...].astype(jnp.bfloat16)
 
     def finish(core):
         def _():
+            if EARLY[core]:
+                ref = ins.at[pl.ds(0, 2), pl.ds(0, EARLY_AT[core][-1])] if EARLY_AT[core][-1] <= ROWS else ins.at[pl.ds(0, 4), pl.ds(0, EARLY_AT[core][-1] // 2)]
+                hop(0, 0, ref, ref, early_send).wait_send()
             for a in range(3):
-                own = ROWS - (EARLY_ROWS if a == 0 else 0)
+                own = sum(n for b, _, n in FIRST[core][EARLY[core] :] if b == a)
                 ring_rows = 2 * (own + 2 * ROWS + (ROWS if core else 0))
                 pushed = ROWS + 2 * (3 * ROWS + (ROWS if core else 0))
                 crossing = sum(p[2] for way in (0, 1) for i, (_, p) in enumerate(BASE[way]) if crosses(way, i) and p[0] == a)
@@ -366,11 +449,15 @@
             pltpu.VMEM((3, ROWS, 2 * LANES), f32),
             pltpu.VMEM((2, EARLY_ROWS, 2 * LANES), f32),
             pltpu.VMEM((8, LANES), f32),
-            pltpu.VMEM((SHARDS, 8, LANES), f32),
+            pltpu.VMEM((8, LANES), f32),
+            pltpu.VMEM((8, LANES), f32),
+            pltpu.VMEM((Z, 8, LANES), f32),
             pltpu.VMEM((SHARDS, LANES), f32),
             pltpu.VMEM((PLANE, SHARDS, LANES), f32),
             pltpu.VMEM((32, LANES), f32),
             dma((5,)),
+            dma,
+            dma,
             dma,
             dma,
             dma,

time: 48.1 us -> 46.9 us (0.975)
  Pallas kernels: 47.3 us -> 46.1 us
    pallas_call x1, Pallas kernels: 44.6 us -> 43.4 us  [per_device(): pl.pallas_call(kernel, name='mix_and_gather', out_shape=(whole, whole, wh...]
where the time goes in v5:
time: 46.9 us; the launch traced here: 46.7 us
  Pallas kernels  46.1 us (98%)
  between operations  0.64 us (1%)
    pallas_call x1, Pallas kernels, per_device(): pl.pallas_call(kernel, name='mix_and_gather', out_shape=(whole, whole, wh...  43.4 us
    pallas_call x1, Pallas kernels, store(): pl.pallas_call(store_kernel, name='store', out_shape=tuple((jax.ShapeDtyp...  2.72 us

profile of v5, /device:TPU:1, one launch (start us, length us, event | category | flops | bytes accessed | tf_op | source)
XLA Modules:
  0.0 46.7 jit_solution(3006334788414468739)
XLA Ops:
  0.6 43.4 %mix_and_gather.1 = (bf16[4096,256]{1,0:T(8,128)(2,1)S(1)}, bf16[4096,256]{1,0:T(8,128)(2,1)S(1)}, bf16[4096,256]{1,0:T(8,128)(2,1)S(1)}, f32[1,256]{1,0:T(1,128...) custom-call(f32[256,256]{1,0:T(8,128)} %oq.1, f32[256,256]{1,0:T(8,128)} %tq.1, ...), custom_call_target="tpu_custom_call" | custom-call | tf_op jit(solution)/shard_map/mix_and_gather/pallas_call | solution.py:439
  44.0 2.7 %store.1 = (bf16[4096,256]{1,0:T(8,128)(2,1)}, bf16[4096,256]{1,0:T(8,128)(2,1)}, bf16[4096,256]{1,0:T(8,128)(2,1)}, f32[1,256]{1,0:T(1,128)}, f32[1,256]{1,0:T(...) custom-call(bf16[4096,256]{1,0:T(8,128)(2,1)S(1)} %get-tuple-element.21.refs_0_, ...), custom_call_target="tpu_custom_call" | custom-call | tf_op jit(solution)/shard_map/store/pallas_call | solution.py:422

commit v6 on v5

--- a/solution.py
+++ b/solution.py
@@ -26,17 +26,22 @@
 PIECE = 16
 
 WHOLE = [(a, 0, ROWS) for a in range(3)]
-FIRST = (
-    [(0, 0, ROWS), (1, 0, ROWS), (2, 0, ROWS)],
-    [(0, 0, HALF), (0, HALF, HALF), (1, 0, ROWS), (2, 0, ROWS)],
+AHEAD = (ROWS, HALF)
+FIRST = tuple(
+    [(0, 0, n)] + [(0, n, ROWS - n)] * (n < ROWS) + [(1, 0, ROWS), (2, 0, ROWS)] for n in AHEAD
 )
 EARLY = (1, 1)
 SPLIT = 128
 CROSS = ((0, SPLIT), (SPLIT, ROWS - SPLIT))
+LESS = 96
+CROSS_TO_0 = ((0, LESS), (LESS, ROWS - LESS))
+LAST_BEFORE_0 = (Z - 1, 1)
 BASE = tuple(
     [(1, p) for p in range(max(len(f) for f in FIRST))]
     + [(2, p) for p in WHOLE]
-    + [(3, p) for p in WHOLE[:2] + [(2, *CROSS[way]), (2, *CROSS[1 - way])]]
+    + [(3, p) for p in WHOLE[:2]]
+    + [(3, p) for p in [(2, *CROSS_TO_0[way]), (2, *CROSS_TO_0[1 - way])] * (way == 1)
+    + [(2, *CROSS[way]), (2, *CROSS[1 - way])] * (way == 0)]
     for way in (0, 1)
 )
 NEAR = sum(d == 1 for d, _ in BASE[0])
@@ -79,23 +84,23 @@
     def greet(device):
         pl.semaphore_signal(barrier, inc=1, device_id=device, device_id_type=MESH)
 
-    @pl.when(c == 0)
-    def _():
-        for target in (ahead, behind):
-            greet({"fsdp_0": target})
-
-    @pl.when(c == 1)
-    def _():
-        for device in far_peers():
-            greet(device)
-
-    greet(partner)
-
     pltpu.make_async_copy(share, share_v, in_sem.at[3]).start()
     for i, src in enumerate((oq, tq, ok, tk, ov, tv)):
         pltpu.make_async_copy(src, ins.at[i], in_sem.at[i // 2]).start()
     for i, src in enumerate((train, step)):
         pltpu.make_async_copy(src, norm_in.at[i], in_sem.at[4]).start()
+
+    @pl.when(c == 0)
+    def _():
+        for target in (ahead, behind):
+            greet({"fsdp_0": target})
+
+    @pl.when(c == 1)
+    def _():
+        for device in far_peers():
+            greet(device)
+
+    greet(partner)
 
     @pl.when(c * PLANE + col == PLANE)
     def _():
@@ -130,11 +135,23 @@
         ref = place(shard, piece)
         return hop(way, i, ref, ref, ici_send.at[piece[0]])
 
-    def last(way, t, d):
+    def last(way, t, d, cross):
         a, other = LAST[t]
         core = lax.rem(c + other, CORES)
-        ref = place(shard_of(way, d, core), (a, *CROSS[way]))
-        return hop(way, STEPS + t, ref, ref, ici_send.at[a])
+        ref = place(shard_of(way, d, core), (a, *cross[way]))
+        return hop(way, t, ref, ref, ici_send.at[a])
+
+    def by_target(way, d, act):
+        special = LAST_BEFORE_0[way] if d == 3 else 0
+        pl.when(z == special)(functools.partial(act, CROSS_TO_0))
+        pl.when(z != special)(functools.partial(act, CROSS))
+
+    def start_last(way, t):
+        by_target(way, 3, lambda cross: last(way, t, 3, cross).start())
+
+    def early_key():
+        a, r, n = FIRST[0][1]
+        return hop(1, 1, mixed.at[a], landed.at[1, pl.ds(EARLY_ROWS, n)], early_send)
 
     def across(ref, a, recv):
         return pltpu.make_async_remote_copy(
@@ -193,6 +210,7 @@
         for i in range(EARLY[0]):
             for way in range(2):
                 early(way, i, 0).start()
+        pl.when(z == 1)(lambda: early_key().start())
         over_chip(total_v, total_v).wait_recv()
 
     @pl.when(c == 1)
@@ -228,15 +246,26 @@
         a, r, n = piece
         put(me, piece, lambda lanes: mixed[a, pl.ds(r, n), lanes])
 
-    for piece in WHOLE:
-        put_own(piece)
+    def own_block(core):
+        def _():
+            late = list(range(EARLY[core], len(FIRST[core])))
+            for k, i in enumerate(late + [None]):
+                if i is not None:
+                    put_own(FIRST[core][i])
+                if k:
+                    for way in range(2):
+                        copy = first(way, late[k - 1], core, me)
+                        if (core, way, late[k - 1]) == (0, 1, 1):
+                            pl.when(z != 1)(copy.start)
+                        else:
+                            copy.start()
+            for i in range(EARLY[core]):
+                put_own(FIRST[core][i])
+
+        return _
+
     for core in range(CORES):
-        @pl.when(c == core)
-        def _():
-            for i in range(EARLY[core], len(FIRST[core])):
-                for way in range(2):
-                    first(way, i, core, me).start()
-
+        pl.when(c == core)(own_block(core))
     for piece in WHOLE:
         push(me, piece).start()
 
@@ -303,7 +332,7 @@
         _, piece = BASE[way][i]
         a = piece[0]
         across(place(shard_of(way, 3, 1 - c), piece), a, cross_recv.at[way, a]).wait_recv()
-        last(way, LAST.index((a, 1)), 3).start()
+        start_last(way, LAST.index((a, 1)))
 
     def near(way, i, core):
         piece = FIRST[core][i]
@@ -312,6 +341,13 @@
         if i < EARLY[core]:
             early(way, i, core).wait_recv()
             put(shard, piece, lambda lanes: landed[way, pl.ds(EARLY_AT[core][i], n), lanes])
+        elif (core, way, i) == (0, 1, 1):
+            @pl.when(z == 0)
+            def _():
+                early_key().wait_recv()
+                put(shard, piece, lambda lanes: landed[1, pl.ds(EARLY_ROWS, n), lanes])
+
+            pl.when(z != 0)(lambda: first(way, i, core, shard).wait_recv())
         else:
             first(way, i, core, shard).wait_recv()
         if r + n == ROWS:
@@ -338,7 +374,7 @@
                 if crosses(way, i):
                     @pl.when(c == 1)
                     def _():
-                        last(way, LAST.index((a, 0)), 3).start()
+                        start_last(way, LAST.index((a, 0)))
                         push(shard, piece).start()
 
                     @pl.when(c == 0)
@@ -354,8 +390,11 @@
     def _():
         for t, (a, other) in enumerate(LAST):
             for way in range(2):
-                last(way, t, 4).wait_recv()
-                push(shard_of(way, 4, lax.rem(c + other, CORES)), (a, *CROSS[way])).start()
+                def take(cross):
+                    last(way, t, 4, cross).wait_recv()
+                    push(shard_of(way, 4, lax.rem(c + other, CORES)), (a, *cross[way])).start()
+
+                by_target(way, 4, take)
 
     @pl.when(c == 1)
     def _():
@@ -382,21 +421,40 @@
 
     norm[...] = norm_f32[...].astype(jnp.bfloat16)
 
+    def sent_early(rows):
+        ref = ins.at[pl.ds(0, rows // HALF), pl.ds(0, HALF)]
+        hop(0, 0, ref, ref, early_send).wait_send()
+
+    def sent_ring(a, rows):
+        ref = rows_of(a, rows)
+        hop(0, 0, ref, ref, ici_send.at[a]).wait_send()
+
     def finish(core):
         def _():
-            if EARLY[core]:
-                ref = ins.at[pl.ds(0, 2), pl.ds(0, EARLY_AT[core][-1])] if EARLY_AT[core][-1] <= ROWS else ins.at[pl.ds(0, 4), pl.ds(0, EARLY_AT[core][-1] // 2)]
-                hop(0, 0, ref, ref, early_send).wait_send()
+            early_rows = EARLY_AT[core][-1]
+            if core == 0:
+                pl.when(z == 1)(functools.partial(sent_early, 2 * early_rows + ROWS))
+                pl.when(z != 1)(functools.partial(sent_early, 2 * early_rows))
+            else:
+                sent_early(2 * early_rows)
             for a in range(3):
                 own = sum(n for b, _, n in FIRST[core][EARLY[core] :] if b == a)
                 ring_rows = 2 * (own + 2 * ROWS + (ROWS if core else 0))
+                fewer = 2 * (SPLIT - LESS)
                 pushed = ROWS + 2 * (3 * ROWS + (ROWS if core else 0))
                 crossing = sum(p[2] for way in (0, 1) for i, (_, p) in enumerate(BASE[way]) if crosses(way, i) and p[0] == a)
                 come = ROWS + 2 * 3 * ROWS + (-crossing if core else 2 * ROWS)
                 ref = rows_of(a, come)
                 across(ref, a, push_recv.at[a]).wait_recv()
-                ref = rows_of(a, ring_rows)
-                hop(0, 0, ref, ref, ici_send.at[a]).wait_send()
+                if core == 1:
+                    pl.when(z == Z - 1)(functools.partial(sent_ring, a, ring_rows - fewer))
+                    pl.when(z == 1)(functools.partial(sent_ring, a, ring_rows + fewer))
+                    pl.when((z > 1) & (z < Z - 1) | (z == 0))(functools.partial(sent_ring, a, ring_rows))
+                elif a == 1:
+                    pl.when(z == 1)(functools.partial(sent_ring, a, ring_rows - ROWS))
+                    pl.when(z != 1)(functools.partial(sent_ring, a, ring_rows))
+                else:
+                    sent_ring(a, ring_rows)
                 ref = rows_of(a, pushed)
                 across(ref, a, push_recv.at[a]).wait_send()
 
@@ -447,7 +505,7 @@
             pltpu.VMEM((1, ROWS), f32),
             pltpu.VMEM((2, 1, PIECE), f32),
             pltpu.VMEM((3, ROWS, 2 * LANES), f32),
-            pltpu.VMEM((2, EARLY_ROWS, 2 * LANES), f32),
+            pltpu.VMEM((2, EARLY_ROWS + ROWS, 2 * LANES), f32),
             pltpu.VMEM((8, LANES), f32),
             pltpu.VMEM((8, LANES), f32),
             pltpu.VMEM((8, LANES), f32),
@@ -466,7 +524,7 @@
             dma,
             dma,
             dma((3,)),
-            dma((2, STEPS + TAIL)),
+            dma((2, STEPS)),
             dma((3,)),
             dma((3,)),
             dma((2, 3)),

time: 46.9 us -> 45.6 us (0.972)
  Pallas kernels: 46.1 us -> 44.9 us
    pallas_call x1, Pallas kernels: 43.4 us -> 42.2 us  [per_device(): pl.pallas_call(kernel, name='mix_and_gather', out_shape=(whole, whole, wh...]
where the time goes in v6:
time: 45.6 us; the launch traced here: 45.5 us
  Pallas kernels  44.9 us (98%)
  between operations  0.64 us (1%)
    pallas_call x1, Pallas kernels, per_device(): pl.pallas_call(kernel, name='mix_and_gather', out_shape=(whole, whole, wh...  42.2 us
    pallas_call x1, Pallas kernels, store(): pl.pallas_call(store_kernel, name='store', out_shape=tuple((jax.ShapeDtyp...  2.72 us

profile of v6, /device:TPU:1, one launch (start us, length us, event | category | flops | bytes accessed | tf_op | source)
XLA Modules:
  0.0 45.5 jit_solution(12624096053103316126)
XLA Ops:
  0.6 42.2 %mix_and_gather.1 = (bf16[4096,256]{1,0:T(8,128)(2,1)S(1)}, bf16[4096,256]{1,0:T(8,128)(2,1)S(1)}, bf16[4096,256]{1,0:T(8,128)(2,1)S(1)}, f32[1,256]{1,0:T(1,128...) custom-call(f32[256,256]{1,0:T(8,128)} %oq.1, f32[256,256]{1,0:T(8,128)} %tq.1, ...), custom_call_target="tpu_custom_call" | custom-call | tf_op jit(solution)/shard_map/mix_and_gather/pallas_call | solution.py:497
  42.8 2.7 %store.1 = (bf16[4096,256]{1,0:T(8,128)(2,1)}, bf16[4096,256]{1,0:T(8,128)(2,1)}, bf16[4096,256]{1,0:T(8,128)(2,1)}, f32[1,256]{1,0:T(1,128)}, f32[1,256]{1,0:T(...) custom-call(bf16[4096,256]{1,0:T(8,128)(2,1)S(1)} %get-tuple-element.21.refs_0_, ...), custom_call_target="tpu_custom_call" | custom-call | tf_op jit(solution)/shard_map/store/pallas_call | solution.py:480

commit v7 on v6

--- a/solution.py
+++ b/solution.py
@@ -31,7 +31,7 @@
     [(0, 0, n)] + [(0, n, ROWS - n)] * (n < ROWS) + [(1, 0, ROWS), (2, 0, ROWS)] for n in AHEAD
 )
 EARLY = (1, 1)
-SPLIT = 128
+SPLIT = 120
 CROSS = ((0, SPLIT), (SPLIT, ROWS - SPLIT))
 LESS = 96
 CROSS_TO_0 = ((0, LESS), (LESS, ROWS - LESS))
@@ -53,7 +53,7 @@
 ANSWER = 4
 PASS = 7
 LAG = 1
-PARTS = 4
+PARTS = 8
 
 
 def kernel(
@@ -354,35 +354,37 @@
             go_on(way, a, 1)
         push(shard, piece).start()
 
+    def arrived(way, i):
+        d, piece = BASE[way][i]
+        if d == 1:
+            for core in range(CORES):
+                if i < len(FIRST[core]):
+                    pl.when(c == core)(functools.partial(near, way, i, core))
+            return
+        a = piece[0]
+        shard = shard_of(way, d, c)
+        ring(way, i, shard).wait_recv()
+        onward(way, i)
+        if crosses(way, i):
+            @pl.when(c == 1)
+            def _():
+                start_last(way, LAST.index((a, 0)))
+                push(shard, piece).start()
+
+            @pl.when(c == 0)
+            def _():
+                across(place(shard, piece), a, cross_recv.at[way, a]).start()
+        else:
+            push(shard, piece).start()
+
     for i in range(STEPS + LAG):
         if i == ANSWER:
             pl.when(c * PLANE + col == PLANE)(answer_all)
         if i == PASS:
             pl.when((col > 0) & (c == 1))(pass_on)
-        if i < STEPS:
-            for way in range(2):
-                d, piece = BASE[way][i]
-                if d == 1:
-                    for core in range(CORES):
-                        if i < len(FIRST[core]):
-                            pl.when(c == core)(functools.partial(near, way, i, core))
-                    continue
-                a = piece[0]
-                shard = shard_of(way, d, c)
-                ring(way, i, shard).wait_recv()
-                onward(way, i)
-                if crosses(way, i):
-                    @pl.when(c == 1)
-                    def _():
-                        start_last(way, LAST.index((a, 0)))
-                        push(shard, piece).start()
-
-                    @pl.when(c == 0)
-                    def _():
-                        across(place(shard, piece), a, cross_recv.at[way, a]).start()
-                else:
-                    push(shard, piece).start()
         for way in range(2):
+            if i < STEPS:
+                arrived(way, i)
             if i >= LAG and crosses(way, i - LAG):
                 pl.when(c == 1)(functools.partial(from_partner, way, i - LAG))
 

time: 45.6 us -> 45.6 us (level)
  no operation moved by 1% of the time
where the time goes in v7:
time: 45.6 us; the launch traced here: 45.5 us
  Pallas kernels  44.9 us (98%)
  between operations  0.64 us (1%)
    pallas_call x1, Pallas kernels, per_device(): pl.pallas_call(kernel, name='mix_and_gather', out_shape=(whole, whole, wh...  42.2 us
    pallas_call x1, Pallas kernels, store(): pl.pallas_call(store_kernel, name='store', out_shape=tuple((jax.ShapeDtyp...  2.7 us

profile of v7, /device:TPU:1, one launch (start us, length us, event | category | flops | bytes accessed | tf_op | source)
XLA Modules:
  0.0 45.5 jit_solution(13808559887353486218)
XLA Ops:
  0.6 42.2 %mix_and_gather.1 = (bf16[4096,256]{1,0:T(8,128)(2,1)S(1)}, bf16[4096,256]{1,0:T(8,128)(2,1)S(1)}, bf16[4096,256]{1,0:T(8,128)(2,1)S(1)}, f32[1,256]{1,0:T(1,128...) custom-call(f32[256,256]{1,0:T(8,128)} %oq.1, f32[256,256]{1,0:T(8,128)} %tq.1, ...), custom_call_target="tpu_custom_call" | custom-call | tf_op jit(solution)/shard_map/mix_and_gather/pallas_call | solution.py:499
  42.8 2.7 %store.1 = (bf16[4096,256]{1,0:T(8,128)(2,1)}, bf16[4096,256]{1,0:T(8,128)(2,1)}, bf16[4096,256]{1,0:T(8,128)(2,1)}, f32[1,256]{1,0:T(1,128)}, f32[1,256]{1,0:T(...) custom-call(bf16[4096,256]{1,0:T(8,128)(2,1)S(1)} %get-tuple-element.21.refs_0_, ...), custom_call_target="tpu_custom_call" | custom-call | tf_op jit(solution)/shard_map/store/pallas_call | solution.py:482

commit v8 on v7

--- a/solution.py
+++ b/solution.py
@@ -182,6 +182,14 @@
                 mixed[a, rows, lanes] = value
                 total = total + jnp.sum(value * value, axis=0, keepdims=True)
             msg[pl.ds(2 * a + j, 1), :] = total
+        if a == 0:
+            @pl.when(c == 0)
+            def _():
+                pl.semaphore_wait(barrier, 3)
+                for i in range(EARLY[0]):
+                    for way in range(2):
+                        early(way, i, 0).start()
+
     pltpu.make_async_copy(norm_in, norm_in, in_sem.at[4]).wait()
     piece = jnp.concatenate(
         [norm_in[0] + norm_in[1], jnp.zeros((1, LANES - PIECE), jnp.float32)], axis=1
@@ -205,11 +213,7 @@
 
     @pl.when(c == 0)
     def _():
-        pl.semaphore_wait(barrier, 3)
         over_chip(msg, both).start()
-        for i in range(EARLY[0]):
-            for way in range(2):
-                early(way, i, 0).start()
         pl.when(z == 1)(lambda: early_key().start())
         over_chip(total_v, total_v).wait_recv()
 

time: 45.6 us -> 45.7 us (level)
  no operation moved by 1% of the time
where the time goes in v8:
time: 45.7 us; the launch traced here: 45.6 us
  Pallas kernels  44.9 us (98%)
  between operations  0.64 us (1%)
    pallas_call x1, Pallas kernels, per_device(): pl.pallas_call(kernel, name='mix_and_gather', out_shape=(whole, whole, wh...  42.2 us
    pallas_call x1, Pallas kernels, store(): pl.pallas_call(store_kernel, name='store', out_shape=tuple((jax.ShapeDtyp...  2.7 us

profile of v8, /device:TPU:1, one launch (start us, length us, event | category | flops | bytes accessed | tf_op | source)
XLA Modules:
  0.0 45.6 jit_solution(18245148623319223820)
XLA Ops:
  0.6 42.2 %mix_and_gather.1 = (bf16[4096,256]{1,0:T(8,128)(2,1)S(1)}, bf16[4096,256]{1,0:T(8,128)(2,1)S(1)}, bf16[4096,256]{1,0:T(8,128)(2,1)S(1)}, f32[1,256]{1,0:T(1,128...) custom-call(f32[256,256]{1,0:T(8,128)} %oq.1, f32[256,256]{1,0:T(8,128)} %tq.1, ...), custom_call_target="tpu_custom_call" | custom-call | tf_op jit(solution)/shard_map/mix_and_gather/pallas_call | solution.py:503
  42.9 2.7 %store.1 = (bf16[4096,256]{1,0:T(8,128)(2,1)}, bf16[4096,256]{1,0:T(8,128)(2,1)}, bf16[4096,256]{1,0:T(8,128)(2,1)}, f32[1,256]{1,0:T(1,128)}, f32[1,256]{1,0:T(...) custom-call(bf16[4096,256]{1,0:T(8,128)(2,1)S(1)} %get-tuple-element.21.refs_0_, ...), custom_call_target="tpu_custom_call" | custom-call | tf_op jit(solution)/shard_map/store/pallas_call | solution.py:486

commit v9 on v7

--- a/solution.py
+++ b/solution.py
@@ -26,11 +26,11 @@
 PIECE = 16
 
 WHOLE = [(a, 0, ROWS) for a in range(3)]
-AHEAD = (ROWS, HALF)
-FIRST = tuple(
-    [(0, 0, n)] + [(0, n, ROWS - n)] * (n < ROWS) + [(1, 0, ROWS), (2, 0, ROWS)] for n in AHEAD
+FIRST = (
+    [(0, 0, ROWS), (1, 0, ROWS), (2, 0, ROWS)],
+    [(0, 0, 32), (0, 32, 96), (0, HALF, HALF), (1, 0, ROWS), (2, 0, ROWS)],
 )
-EARLY = (1, 1)
+EARLY = (1, 2)
 SPLIT = 120
 CROSS = ((0, SPLIT), (SPLIT, ROWS - SPLIT))
 LESS = 96
@@ -216,11 +216,17 @@
     @pl.when(c == 1)
     def _():
         pl.semaphore_wait(barrier, Z + (col + PLANE - 1) // PLANE)
+        def first_rows():
+            for way in range(2):
+                early(way, 0, 1).start()
+
+        pl.when(z >= Z // 2)(first_rows)
         over_chip(msg, both).wait_recv()
         both[...] = both[...] + msg[...]
         for device in far_peers():
             message(device, both, sums.at[z]).start()
-        for i in range(EARLY[1]):
+        pl.when(z < Z // 2)(first_rows)
+        for i in range(1, EARLY[1]):
             for way in range(2):
                 early(way, i, 1).start()
         sums[pl.ds(z, 1)] = both[...][None]

time: 45.6 us -> 45.6 us (level)
  no operation moved by 1% of the time
where the time goes in v9:
time: 45.6 us; the launch traced here: 45.5 us
  Pallas kernels  44.9 us (98%)
  between operations  0.64 us (1%)
    pallas_call x1, Pallas kernels, per_device(): pl.pallas_call(kernel, name='mix_and_gather', out_shape=(whole, whole, wh...  42.2 us
    pallas_call x1, Pallas kernels, store(): pl.pallas_call(store_kernel, name='store', out_shape=tuple((jax.ShapeDtyp...  2.7 us

profile of v9, /device:TPU:1, one launch (start us, length us, event | category | flops | bytes accessed | tf_op | source)
XLA Modules:
  0.0 45.5 jit_solution(12718672958837503028)
XLA Ops:
  0.6 42.2 %mix_and_gather.1 = (bf16[4096,256]{1,0:T(8,128)(2,1)S(1)}, bf16[4096,256]{1,0:T(8,128)(2,1)S(1)}, bf16[4096,256]{1,0:T(8,128)(2,1)S(1)}, f32[1,256]{1,0:T(1,128...) custom-call(f32[256,256]{1,0:T(8,128)} %oq.1, f32[256,256]{1,0:T(8,128)} %tq.1, ...), custom_call_target="tpu_custom_call" | custom-call | tf_op jit(solution)/shard_map/mix_and_gather/pallas_call | solution.py:505
  42.8 2.7 %store.1 = (bf16[4096,256]{1,0:T(8,128)(2,1)}, bf16[4096,256]{1,0:T(8,128)(2,1)}, bf16[4096,256]{1,0:T(8,128)(2,1)}, f32[1,256]{1,0:T(1,128)}, f32[1,256]{1,0:T(...) custom-call(bf16[4096,256]{1,0:T(8,128)(2,1)S(1)} %get-tuple-element.21.refs_0_, ...), custom_call_target="tpu_custom_call" | custom-call | tf_op jit(solution)/shard_map/store/pallas_call | solution.py:488
